TPU v7x, 128 devices: a whole 4x4x4 slice. The times are simulated.
128 devices in a mesh: ep: 8 (over y, core), fs: 16 (over z, x).
Axes of the slice: x: 4, y: 4, z: 4, core: 2. Of those that a mesh axis runs over, the one named last changes fastest.
Arguments:
- grads: bfloat16 [8, 8, 256, 14336], P('ep', None, 'fs'), may hold values from -64 to 64
- counts: int32 [8, 8], replicated, may hold values from 16 to 2047
- weight: bfloat16 [8, 256, 14336], P('ep', 'fs'), may hold values from -3 to 3
- mom: float32 [8, 256, 14336], P('ep', 'fs'), may hold values from -64 to 64
- second: float32 [8, 256, 14336], P('ep', 'fs'), may hold values from 0.1 to 10
- in_weight: float32 [6, 32], replicated, may hold values from -2.5 to 2.5
- in_bias: float32 [32], replicated, may hold values from -3 to 3
- out_weight: float32 [32, 2], replicated, may hold values from -1 to 1
- out_bias: float32 [2], replicated, may hold values from -3 to 3
Outputs:
- new_weight: bfloat16 [8, 256, 14336], P('ep')
- new_mom: float32 [8, 256, 14336], P('ep', 'fs')
- new_second: float32 [8, 256, 14336], P('ep', 'fs')
All inputs are finite; a program needn't handle non-finite values.
Results may differ from a plain program's by a relative error of at most 0.0019.
Values may be sent and summed in bfloat16 or wider, within the bound.
A program may use at most 64 MiB of HBM per device.

v0:
```python
import jax
import jax.numpy as jnp
from jax import lax
from jax.sharding import PartitionSpec as P

MOMENTUM_DECAY = 0.9
SECOND_DECAY = 0.99
NORM_EPS = 1e-06
ROOT_EPS = 1e-08
STEP_SCALE = 0.2
EXP_SCALE = 0.5


def from_everyone(value, axis):
    copies = jnp.broadcast_to(value, (lax.axis_size(axis), *value.shape))
    return lax.all_to_all(copies, axis, split_axis=0, concat_axis=0, tiled=True)


def of_everyone(value, axis):
    return from_everyone(value, axis).sum(axis=0)


def in_one(arrays, axis):
    line, at, done = (jnp.concatenate([a.reshape(-1) for a in arrays]), 0, [])
    so_far = of_everyone(line, axis)
    for a in arrays:
        done.append(so_far[at : at + a.size].reshape(a.shape))
        at += a.size
    return tuple(done)


def learned_step(
    gradient,
    mom_next,
    second_next,
    weight,
    grad_norm,
    mom_norm,
    in_weight,
    in_bias,
    out_weight,
    out_bias,
):
    inv_root = lax.rsqrt(second_next + ROOT_EPS)
    features = jnp.stack(
        [
            gradient / grad_norm,
            mom_next / mom_norm,
            mom_next * inv_root,
            gradient * inv_root,
            weight.astype(jnp.float32),
            jnp.broadcast_to(jnp.log(mom_norm), gradient.shape),
        ]
    )
    hidden = jax.nn.relu(
        jnp.einsum("fh,fab->hab", in_weight, features, precision=lax.Precision.HIGHEST)
        + in_bias[:, None, None]
    )
    outputs = (
        jnp.einsum("hk,hab->kab", out_weight, hidden, precision=lax.Precision.HIGHEST)
        + out_bias[:, None, None]
    )
    update = STEP_SCALE * outputs[0] * jnp.exp(EXP_SCALE * outputs[1])
    return (weight.astype(jnp.float32) - update).astype(jnp.bfloat16)


def add_sources(arrived):
    return jnp.sum(arrived.astype(jnp.float32), axis=0)


def per_device(grads, counts, weight, mom, second, in_weight, in_bias, out_weight, out_bias):
    source = lax.axis_index("ep")
    counts_f = counts.astype(jnp.float32)
    totals = jnp.sum(counts_f, axis=0)
    share_row = lax.dynamic_index_in_dim(counts_f, source, 0, keepdims=False) / totals
    weighted = share_row[None, :, None, None] * grads.astype(jnp.float32)
    outgoing = weighted.astype(jnp.bfloat16)
    gradient = add_sources(lax.all_to_all(outgoing, "ep", split_axis=1, concat_axis=0, tiled=True))[
        0
    ]
    mom_here = mom[0]
    second_here = second[0]
    mom_next = MOMENTUM_DECAY * mom_here + (1.0 - MOMENTUM_DECAY) * gradient
    second_next = SECOND_DECAY * second_here + (1.0 - SECOND_DECAY) * gradient * gradient
    entries = gradient.shape[0] * gradient.shape[1] * lax.axis_size("fs")
    grad_sq, mom_sq = in_one((jnp.sum(gradient * gradient), jnp.sum(mom_next * mom_next)), "fs")
    grad_norm = jnp.sqrt(grad_sq / entries + NORM_EPS)
    mom_norm = jnp.sqrt(mom_sq / entries + NORM_EPS)
    width = gradient.shape[1]

    def block_step(items):
        grad_block, mom_block, second_block, weight_block = items
        return learned_step(
            grad_block,
            mom_block,
            second_block,
            weight_block,
            grad_norm,
            mom_norm,
            in_weight,
            in_bias,
            out_weight,
            out_bias,
        )

    blocks = lax.map(
        block_step,
        (
            gradient.reshape(-1, 2, width),
            mom_next.reshape(-1, 2, width),
            second_next.reshape(-1, 2, width),
            weight[0].reshape(-1, 2, width),
        ),
    )
    updated = blocks.reshape(gradient.shape)
    gathered = lax.all_gather(updated[None], "fs", axis=1, tiled=True)
    return (gathered, mom_next[None], second_next[None])


def solution(mesh):
    in_specs = (
        P("ep", None, "fs", None),
        P(),
        P("ep", "fs", None),
        P("ep", "fs", None),
        P("ep", "fs", None),
        P(),
        P(),
        P(),
        P(),
    )
    out_specs = (P("ep", None, None), P("ep", "fs", None), P("ep", "fs", None))
    return jax.shard_map(
        per_device, mesh=mesh, in_specs=in_specs, out_specs=out_specs, check_vma=False
    )
```

profile of v0, /device:TPU:0, one launch (start us, length us, event | category | flops | bytes accessed | tf_op | source)
XLA Modules:
  0.0 245.7 jit_solution(12678078749305325285)
XLA Ops:
  8.6 4.7 %multiply_convert_fusion = bf16[1,8,16,14336]{3,2,0,1:T(8,128)(2,1)} fusion(bf16[1,8,16,14336]{3,2,1,0:T(8,128)(2,1)} %param.11, f32[8]{0:T(128)S(1)} %bitcast_divide_fusion), kind=kLoop, calls=%fused_computation.22 | loop fusion | flops 5505024 | bytes 7340064 | tf_op jit(solution)/shard_map/convert_element_type | solution.py:77
  13.3 4.7 %all-to-all-start = ((bf16[1,8,16,14336]{3,2,0,1:T(8,128)(2,1)}), bf16[1,8,16,14336]{3,2,0,1:T(8,128)(2,1)}, u32[]{:S(2)}, u32[]{:S(2)}) async-start(bf16[1,8,16,14336]{3,2,0,1:T(8,128)(2,1)} %multiply_convert_fusion), calls=%async_computation | async-start | bytes 7340032 | tf_op jit(solution)/shard_map/all_to_all | solution.py:78
  18.3 43.8 %all-to-all-done = bf16[1,8,16,14336]{3,2,0,1:T(8,128)(2,1)} async-done(((bf16[1,8,16,14336]{3,2,0,1:T(8,128)(2,1)}), bf16[1,8,16,14336]{3,2,0,1:T(8,128)(2,1)}, u32[]{:S(2)}, u32[]{:S(2)}) %all-to-all-start) | async-done | bytes 3670048 | tf_op jit(solution)/shard_map/all_to_all | solution.py:78
  62.1 2.6 %convert_reduce_fusion = f32[16,14336]{1,0:T(8,128)S(1)} fusion(bf16[1,8,16,14336]{3,2,0,1:T(8,128)(2,1)} %all-to-all-done), kind=kLoop, calls=%fused_computation.21 | loop fusion | flops 3440640 | bytes 4587520 | tf_op jit(solution)/shard_map/reduce_sum | solution.py:68
  69.0 7.9 %all-to-all-start.1 = ((f32[16,1,2]{2,1,0:T(1,128)}), f32[16,1,2]{2,1,0:T(1,128)S(1)}, u32[]{:S(2)}, u32[]{:S(2)}) async-start(f32[16,1,2]{2,1,0:T(1,128)} %broadcast_in_dim.18), calls=%async_computation.1 | async-start | bytes 16384 | tf_op jit(solution)/shard_map/all_to_all | solution.py:16
  77.2 2.9 %fusion.10 = (f32[1,16,14336]{2,1,0:T(8,128)}, f32[1,16,14336]{2,1,0:T(8,128)}, f32[1,16,14336]{2,1,0:T(8,128)}, f32[1,16,14336]{2,1,0:T(8,128)S(1)}) fusion(f32[16,14336]{1,0:T(8,128)S(1)} %convert_reduce_fusion, f32[1,16,14336]{2,1,0:T(8,128)} %param.15, f32[1,16,14336]{2,1,0:T(8,128)S(1)} %copy-done), kind=kLoop, calls=%fused_computation.26 | loop fusion | flops 1605632 | bytes 6422528 | tf_op jit(solution)/shard_map/add | solution.py:84
  82.3 4.1 %fusion.9 = (f32[8,2,14336]{2,0,1:T(8,128)S(1)}, f32[8,2,14336]{2,0,1:T(8,128)}, f32[8,2,14336]{2,0,1:T(8,128)}) fusion(f32[8,2,14336]{2,1,0:T(2,128)S(1)} %mul.131, f32[8,2,14336]{2,1,0:T(2,128)} %reshape_squeeze.7, f32[8,2,14336]{2,1,0:T(2,128)S(1)} %mul.126), kind=kLoop, calls=%fused_computation.25 | loop fusion | flops 1146880 | bytes 5505024 | tf_op jit(solution)/shard_map/add | solution.py:84
  88.3 75.6 %while.11 = (s32[]{:T(128)}, bf16[8,2,14336]{2,1,0:T(2,128)(2,1)}, bf16[8,2,14336]{2,1,0:T(2,128)(2,1)S(1)}, f32[8,2,14336]{2,0,1:T(8,128)}, f32[]{:T(128)}, /*i...) while((s32[]{:T(128)}, bf16[8,2,14336]{2,1,0:T(2,128)(2,1)}, ...), condition=%wide.region_6.7_spmd, body=%wide.region_5.6_spmd.sunk | while | flops 90316800 | bytes 11298093 | solution.py:106
  91.5 3.2 %fusion.28 = f32[32,2,14336]{2,0,1:T(8,128)S(1)} fusion(f32[6,2,14336]{2,0,1:T(8,128)S(1)} %stack.4, f32[32]{0:T(128)S(1)} %get-tuple-element.350, f32[6,32]{1,0:T(8,128)S(1)} %get-tuple-element.349), kind=kOutput, calls=%fused_computation.2.clone.1 | convolution fusion | flops 67895296 | bytes 4359040 | tf_op jit(solution)/shard_map/while/body/eval_jaxpr/fh,fab->hab/dot_general | solution.py:56
  94.7 2.1 fusion.29
  100.9 3.2 %fusion.28 = f32[32,2,14336]{2,0,1:T(8,128)S(1)} fusion(f32[6,2,14336]{2,0,1:T(8,128)S(1)} %stack.4, f32[32]{0:T(128)S(1)} %get-tuple-element.350, f32[6,32]{1,0:T(8,128)S(1)} %get-tuple-element.349), kind=kOutput, calls=%fused_computation.2.clone.1 | convolution fusion | flops 67895296 | bytes 4359040 | tf_op jit(solution)/shard_map/while/body/eval_jaxpr/fh,fab->hab/dot_general | solution.py:56
  104.1 2.1 fusion.29
  110.4 3.2 %fusion.28 = f32[32,2,14336]{2,0,1:T(8,128)S(1)} fusion(f32[6,2,14336]{2,0,1:T(8,128)S(1)} %stack.4, f32[32]{0:T(128)S(1)} %get-tuple-element.350, f32[6,32]{1,0:T(8,128)S(1)} %get-tuple-element.349), kind=kOutput, calls=%fused_computation.2.clone.1 | convolution fusion | flops 67895296 | bytes 4359040 | tf_op jit(solution)/shard_map/while/body/eval_jaxpr/fh,fab->hab/dot_general | solution.py:56
  113.6 2.1 fusion.29
  119.8 3.2 %fusion.28 = f32[32,2,14336]{2,0,1:T(8,128)S(1)} fusion(f32[6,2,14336]{2,0,1:T(8,128)S(1)} %stack.4, f32[32]{0:T(128)S(1)} %get-tuple-element.350, f32[6,32]{1,0:T(8,128)S(1)} %get-tuple-element.349), kind=kOutput, calls=%fused_computation.2.clone.1 | convolution fusion | flops 67895296 | bytes 4359040 | tf_op jit(solution)/shard_map/while/body/eval_jaxpr/fh,fab->hab/dot_general | solution.py:56
  123.0 2.1 fusion.29
  129.3 3.2 %fusion.28 = f32[32,2,14336]{2,0,1:T(8,128)S(1)} fusion(f32[6,2,14336]{2,0,1:T(8,128)S(1)} %stack.4, f32[32]{0:T(128)S(1)} %get-tuple-element.350, f32[6,32]{1,0:T(8,128)S(1)} %get-tuple-element.349), kind=kOutput, calls=%fused_computation.2.clone.1 | convolution fusion | flops 67895296 | bytes 4359040 | tf_op jit(solution)/shard_map/while/body/eval_jaxpr/fh,fab->hab/dot_general | solution.py:56
  132.5 2.1 fusion.29
  138.7 3.2 %fusion.28 = f32[32,2,14336]{2,0,1:T(8,128)S(1)} fusion(f32[6,2,14336]{2,0,1:T(8,128)S(1)} %stack.4, f32[32]{0:T(128)S(1)} %get-tuple-element.350, f32[6,32]{1,0:T(8,128)S(1)} %get-tuple-element.349), kind=kOutput, calls=%fused_computation.2.clone.1 | convolution fusion | flops 67895296 | bytes 4359040 | tf_op jit(solution)/shard_map/while/body/eval_jaxpr/fh,fab->hab/dot_general | solution.py:56
  141.9 2.1 fusion.29
  148.2 3.2 %fusion.28 = f32[32,2,14336]{2,0,1:T(8,128)S(1)} fusion(f32[6,2,14336]{2,0,1:T(8,128)S(1)} %stack.4, f32[32]{0:T(128)S(1)} %get-tuple-element.350, f32[6,32]{1,0:T(8,128)S(1)} %get-tuple-element.349), kind=kOutput, calls=%fused_computation.2.clone.1 | convolution fusion | flops 67895296 | bytes 4359040 | tf_op jit(solution)/shard_map/while/body/eval_jaxpr/fh,fab->hab/dot_general | solution.py:56
  157.6 3.2 %fusion.28 = f32[32,2,14336]{2,0,1:T(8,128)S(1)} fusion(f32[6,2,14336]{2,0,1:T(8,128)S(1)} %stack.4, f32[32]{0:T(128)S(1)} %get-tuple-element.350, f32[6,32]{1,0:T(8,128)S(1)} %get-tuple-element.349), kind=kOutput, calls=%fused_computation.2.clone.1 | convolution fusion | flops 67895296 | bytes 4359040 | tf_op jit(solution)/shard_map/while/body/eval_jaxpr/fh,fab->hab/dot_general | solution.py:56
  165.9 66.1 %all-gather.2.cloned.1.call-done = bf16[1,256,14336]{2,1,0:T(8,128)(2,1)} async-done(((bf16[1,16,14336]{2,1,0:T(8,128)(2,1)}), bf16[1,256,14336]{2,1,0:T(8,128)(2,1)}) %all-gather.2.cloned.1.call-update) | async-done | bytes 7340048 | tf_op jit(solution)/shard_map/all_gather | solution.py:116
  231.9 6.9 %copy.86 = bf16[1,256,14336]{2,1,0:T(8,128)(2,1)} copy(bf16[1,256,14336]{2,1,0:T(8,128)(2,1)} %all-gather.2.cloned.1.call-done) | data formatting | bytes 14680064
  (87 shorter events, 48.4 us)
Async XLA Ops:
  13.2 4.7 %copy-start.1 = (bf16[1,16,14336]{2,1,0:T(8,128)(2,1)S(1)}, bf16[1,16,14336]{2,1,0:T(8,128)(2,1)}, u32[]{:S(2)}) copy-start(bf16[1,16,14336]{2,1,0:T(8,128)(2,1)} %param.13) | copy-start | bytes 1376260
  13.3 48.8 %all-to-all-start = ((bf16[1,8,16,14336]{3,2,0,1:T(8,128)(2,1)}), bf16[1,8,16,14336]{3,2,0,1:T(8,128)(2,1)}, u32[]{:S(2)}, u32[]{:S(2)}) async-start(bf16[1,8,16,14336]{3,2,0,1:T(8,128)(2,1)} %multiply_convert_fusion), calls=%async_computation | async-start | bytes 7340032 | tf_op jit(solution)/shard_map/all_to_all | solution.py:78
  18.0 48.2 %copy-start = (f32[1,16,14336]{2,1,0:T(8,128)S(1)}, f32[1,16,14336]{2,1,0:T(8,128)}, u32[]{:S(2)}) copy-start(f32[1,16,14336]{2,1,0:T(8,128)} %param.14) | copy-start | bytes 2752516
  69.0 17.4 %all-to-all-start.1 = ((f32[16,1,2]{2,1,0:T(1,128)}), f32[16,1,2]{2,1,0:T(1,128)S(1)}, u32[]{:S(2)}, u32[]{:S(2)}) async-start(f32[16,1,2]{2,1,0:T(1,128)} %broadcast_in_dim.18), calls=%async_computation.1 | async-start | bytes 16384 | tf_op jit(solution)/shard_map/all_to_all | solution.py:16
  76.9 155.0 %all-gather.2.cloned.1.call-start = ((), (), s32[]{:S(2)}) async-start(), calls=%async_computation.2 | async-start | bytes 7798784 | tf_op jit(solution)/shard_map/all_gather | solution.py:116
  81.7 6.5 %copy-start.2 = (f32[6,32]{1,0:T(8,128)S(1)}, f32[6,32]{1,0:T(8,128)}, u32[]{:S(2)}) copy-start(f32[6,32]{1,0:T(8,128)} %param.16) | copy-start | bytes 2308
  81.8 6.5 %copy-start.3 = (f32[32,2]{0,1:T(2,128)S(1)}, f32[32,2]{0,1:T(2,128)}, u32[]{:S(2)}) copy-start(f32[32,2]{0,1:T(2,128)} %param.18) | copy-start | bytes 772
  81.8 6.5 %copy-start.4 = (f32[32]{0:T(128)S(1)}, f32[32]{0:T(128)}, u32[]{:S(2)}) copy-start(f32[32]{0:T(128)} %param.17) | copy-start | bytes 388
  81.8 6.5 %copy-start.5 = (f32[2]{0:T(128)S(1)}, f32[2]{0:T(128)}, u32[]{:S(2)}) copy-start(f32[2]{0:T(128)} %param.19) | copy-start | bytes 28
Sparse Core Ops, SparseCore 0:
  166.0 65.9 all-gather.1
where the time goes:
time: 247 us; the launch traced here: 246 us
  waiting for transfers between devices  110 us (45%)
  matrix products  42 us (17%)
  other arithmetic  35.8 us (14%)
  local copies, waits for them, and re-layouts  29.4 us (12%)
  between operations  15.4 us (6%)
  starting transfers between devices  12.8 us (5%)
    all_gather x1, waiting for transfers between devices, per_device(): gathered = lax.all_gather(updated[None], 'fs', axis=1, tiled=True)  66.1 us
    all_to_all x1, waiting for transfers between devices, per_device(): lax.all_to_all(outgoing, 'ep', split_axis=1, concat_axis=0, tiled=True)  43.8 us
    dot_general x8, matrix products, learned_step(): jnp.einsum('fh,fab->hab', in_weight, features, precision=lax.Precision.HI...  25.6 us
    dot_general x8, matrix products, learned_step(): jnp.einsum('hk,hab->kab', out_weight, hidden, precision=lax.Precision.HIG...  16.4 us
    mul x8, other arithmetic, learned_step(): gradient * inv_root  14.7 us
    another operation x8, local copies, waits for them, and re-layouts, learned_step(): jnp.stack([gradient / grad_norm, mom_next / mom_norm, mom_next * inv_root...  8.98 us
    all_to_all x1, starting transfers between devices, from_everyone(): return lax.all_to_all(copies, axis, split_axis=0, concat_axis=0, tiled=True)  7.88 us
    unnamed x13, local copies, waits for them, and re-layouts  6.93 us
  transfers between devices with their start and end apart: 3, of which 2 were waited for; matrix products, arithmetic and copies ran while one was open for 4% of the time, Pallas kernels for 0%

commit v1 on v0

v1 whole, which is shorter than its diff:
```python
import functools

import jax
import jax.numpy as jnp
from jax import lax
from jax.experimental import pallas as pl
from jax.experimental.pallas import tpu as pltpu
from jax.sharding import PartitionSpec as P

MOMENTUM_DECAY = 0.9
SECOND_DECAY = 0.99
NORM_EPS = 1e-06
ROOT_EPS = 1e-08
STEP_SCALE = 0.2
EXP_SCALE = 0.5

ROWS = 16
LANE = 128
CHUNKS = 7
LAG = (1, 2, 3)
MESH = pl.DeviceIdType.MESH
F32 = jnp.float32
BF16 = jnp.bfloat16

CODE_POWER = 6.0
CODE_SCALE = 2.0**14


def encode(x):
    y = jnp.exp(CODE_POWER * jnp.log(jnp.abs(x) * CODE_SCALE))
    return jnp.where(x < 0, -y, y).astype(BF16)


def decode(code):
    v = code.astype(F32)
    m = jnp.exp(jnp.log(jnp.abs(v)) * (1.0 / CODE_POWER)) * (1.0 / CODE_SCALE)
    return jnp.where(v < 0, -m, m)


def loop(n, body, unroll=1):
    def step(i, carry):
        body(i)
        return carry

    lax.fori_loop(0, n, step, 0, unroll=unroll)


def kernel(
    width,
    counts,
    in_weight,
    in_bias,
    out_weight,
    out_bias,
    grads_hbm,
    weight_hbm,
    mom_hbm,
    second_hbm,
    gathered,
    new_mom,
    new_second,
    grads,
    weight,
    mom,
    second,
    to_pair,
    from_pair,
    far_out,
    far_in,
    up_out,
    up_in,
    down_out,
    down_in,
    own_sum,
    part_sum,
    shares,
    table,
    sums_out,
    sums_in,
    sums_out_z,
    sums_in_z,
    load_sem,
    pair_send,
    pair_recv,
    ring_send,
    ring_recv,
    sums_send,
    sums_recv,
    gather_send,
    gather_recv,
):
    wc = width // CHUNKS
    half = wc // 2
    quarter = wc // 4
    ep = lax.axis_index("ep")
    fs = lax.axis_index("fs")
    y, core = ep // 2, ep % 2
    z, x = fs // 4, fs % 4

    def on_y(step):
        return {"ep": ((y + step) % 4) * 2 + core}

    def on_x(step):
        return {"fs": z * 4 + (x + step) % 4}

    def on_z(step):
        return {"fs": ((z + step) % 4) * 4 + x}

    partner = {"ep": y * 2 + (1 - core)}

    def cols(k, start=0, size=None):
        return pl.ds(pl.multiple_of(k * wc + start, LANE), wc if size is None else size)

    def grads_load(k):
        return pltpu.make_async_copy(
            grads_hbm.at[0, :, :, cols(k)], grads.at[:, :, cols(k)], load_sem.at[k]
        )

    state_loads = [
        pltpu.make_async_copy(src.at[0], dst, load_sem.at[CHUNKS + i])
        for i, (src, dst) in enumerate(
            ((weight_hbm, weight), (mom_hbm, mom), (second_hbm, second))
        )
    ]
    loop(CHUNKS, lambda k: grads_load(k).start())
    for load in state_loads:
        load.start()

    barrier = pltpu.get_barrier_semaphore()
    peers = [partner, on_y(1), on_y(3)]
    peers += [on_x(1), on_x(2), on_x(3), on_z(1), on_z(2), on_z(3)]
    for peer in peers:
        pl.semaphore_signal(barrier, inc=1, device_id=peer, device_id_type=MESH)

    counted = counts[...].astype(F32)
    share_table = counted / jnp.sum(counted, axis=0, keepdims=True)
    row_id = lax.broadcasted_iota(jnp.int32, (8, 8), 0)
    col_id = lax.broadcasted_iota(jnp.int32, (8, 8), 1)
    for i in range(8):
        c = core if i >= 4 else 1 - core
        e = ((y + i) % 4) * 2 + c
        picked = jnp.where((row_id == ep) & (col_id == e), share_table, 0.0)
        one = jnp.sum(jnp.sum(picked, axis=1, keepdims=True), axis=0, keepdims=True)
        shares[i] = jnp.broadcast_to(one, (ROWS, LANE))

    for i in range(5):
        loop(32, lambda j, i=i: spread(table, j, i, in_weight[i, j]))
    for i in range(2):
        loop(32, lambda j, i=i: spread(table, j, 6 + i, out_weight[i, j]))

    pl.semaphore_wait(barrier, len(peers))

    tiles = wc // LANE
    half_tiles = half // LANE

    def tile(k, t):
        return pl.ds(pl.multiple_of(k * wc + t * LANE, LANE), LANE)

    def pair_copy(k):
        return pltpu.make_async_remote_copy(
            src_ref=to_pair.at[:, :, cols(k)],
            dst_ref=from_pair.at[:, :, cols(k)],
            send_sem=pair_send.at[k],
            recv_sem=pair_recv.at[k],
            device_id=partner,
            device_id_type=MESH,
        )

    def weigh(k):
        grads_load(k).wait()

        def body(t):
            at = tile(k, t)
            for i in range(4):
                e = ((y + i) % 4) * 2 + (1 - core)
                to_pair[i, :, at] = (grads[e, :, at].astype(F32) * shares[i]).astype(BF16)

        loop(tiles, body, unroll=4)
        pair_copy(k).start()

    loop(CHUNKS, weigh)

    def ring_copy(src, dst, kind, k, start, size, device):
        return pltpu.make_async_remote_copy(
            src_ref=src.at[:, cols(k, start, size)],
            dst_ref=dst.at[:, cols(k, start, size)],
            send_sem=ring_send.at[kind, k],
            recv_sem=ring_recv.at[kind, k],
            device_id=device,
            device_id_type=MESH,
        )

    def far_a(k):
        return ring_copy(far_out, far_in, 0, k, 0, half, on_y(1))

    def far_b(k):
        return ring_copy(far_out, far_in, 1, k, half, half, on_y(3))

    def up_a(k):
        return ring_copy(up_out, up_in, 2, k, 0, half, on_y(1))

    def up_b(k):
        return ring_copy(up_out, up_in, 3, k, half, half, on_y(1))

    def down_a(k):
        return ring_copy(down_out, down_in, 4, k, 0, half, on_y(3))

    def down_b(k):
        return ring_copy(down_out, down_in, 5, k, half, half, on_y(3))

    def pair_sum(i, at):
        e = ((y + i) % 4) * 2 + core
        mine = (grads[e, :, at].astype(F32) * shares[4 + i]).astype(BF16).astype(F32)
        return mine + from_pair[i, :, at].astype(F32)

    def sum_pairs(k):
        pair_copy(k).wait_recv()

        def far(t):
            at = tile(k, t)
            far_out[:, at] = encode(pair_sum(2, at))

        loop(tiles, far, unroll=2)
        far_a(k).start()
        far_b(k).start()

        def first(t):
            a, b = tile(k, t), tile(k, t + half_tiles)
            down_out[:, a] = encode(pair_sum(3, a))
            up_out[:, b] = encode(pair_sum(1, b))

        loop(half_tiles, first, unroll=2)
        up_b(k).start()
        down_a(k).start()

        def rest(t):
            a, b = tile(k, t), tile(k, t + half_tiles)
            part_sum[:, a] = pair_sum(1, a)
            part_sum[:, b] = pair_sum(3, b)
            own_sum[:, a] = pair_sum(0, a)
            own_sum[:, b] = pair_sum(0, b)

        loop(half_tiles, rest, unroll=2)

    loop(CHUNKS, sum_pairs)

    def pass_on(k):
        far_a(k).wait_recv()

        def up(t):
            at = tile(k, t)
            up_out[:, at] = encode(part_sum[:, at] + decode(far_in[:, at]))

        loop(half_tiles, up, unroll=2)
        up_a(k).start()
        far_b(k).wait_recv()

        def down(t):
            at = tile(k, t + half_tiles)
            down_out[:, at] = encode(part_sum[:, at] + decode(far_in[:, at]))

        loop(half_tiles, down, unroll=2)
        down_b(k).start()

    loop(CHUNKS, pass_on)

    for load in state_loads:
        load.wait()

    def moments(k, sums):
        up_a(k).wait_recv()
        up_b(k).wait_recv()
        down_a(k).wait_recv()
        down_b(k).wait_recv()

        def body(t, sums):
            grad_sq, mom_sq = sums
            at = tile(k, t)
            gradient = own_sum[:, at] + decode(up_in[:, at]) + decode(down_in[:, at])
            mom_next = MOMENTUM_DECAY * mom[:, at] + (1.0 - MOMENTUM_DECAY) * gradient
            squared = gradient * gradient
            own_sum[:, at] = gradient
            new_mom[:, at] = mom_next
            new_second[:, at] = SECOND_DECAY * second[:, at] + (1.0 - SECOND_DECAY) * squared
            return grad_sq + squared, mom_sq + mom_next * mom_next

        return lax.fori_loop(0, tiles, body, sums, unroll=2)

    zero = jnp.zeros((ROWS, LANE), F32)
    grad_sq, mom_sq = lax.fori_loop(0, CHUNKS, moments, (zero, zero))

    sums_out[0] = grad_sq[0:8] + grad_sq[8:16]
    sums_out[1] = mom_sq[0:8] + mom_sq[8:16]

    def sums_copy(src, dst, stage, i, device):
        return pltpu.make_async_remote_copy(
            src_ref=src,
            dst_ref=dst.at[i - 1],
            send_sem=sums_send.at[stage, i - 1],
            recv_sem=sums_recv.at[stage, i - 1],
            device_id=device,
            device_id_type=MESH,
        )

    for stage, (src, dst, toward) in enumerate(
        ((sums_out, sums_in, on_x), (sums_out_z, sums_in_z, on_z))
    ):
        for i in (1, 2, 3):
            sums_copy(src, dst, stage, i, toward(i)).start()
        for i in (1, 2, 3):
            sums_copy(src, dst, stage, i, toward(i)).wait_recv()
        total = src[...] + dst[0] + dst[1] + dst[2]
        if stage == 0:
            sums_out_z[...] = total

    entries = float(ROWS * width * 16)
    whole = jnp.sum(jnp.sum(total, axis=2, keepdims=True), axis=1, keepdims=True)
    grad_var = whole[0] / entries + NORM_EPS
    mom_var = whole[1] / entries + NORM_EPS
    inv_grad = jnp.broadcast_to(lax.rsqrt(grad_var), (8, LANE))
    inv_mom = jnp.broadcast_to(lax.rsqrt(mom_var), (8, LANE))
    log_mom = jnp.broadcast_to(0.5 * jnp.log(mom_var), (8, LANE))

    loop(32, lambda j: offset(table, j, in_weight[5, j], in_bias[j], log_mom))
    direction_bias = jnp.full((8, LANE), out_bias[0], F32)
    magnitude_bias = jnp.full((8, LANE), out_bias[1], F32)

    my_rows = pl.ds(pl.multiple_of(fs * ROWS, ROWS), ROWS)

    def network(k):
        def body(t):
            ats = [tile(k, 2 * t), tile(k, 2 * t + 1)]
            feats = []
            weights = []
            for at in ats:
                w16 = weight[:, at].astype(F32)
                for r in (0, 8):
                    rows = slice(r, r + 8)
                    g = own_sum[rows, at]
                    m = new_mom[rows, at]
                    inv_root = lax.rsqrt(new_second[rows, at] + ROOT_EPS)
                    w = w16[rows]
                    weights.append(w)
                    feats.append((g * inv_grad, m * inv_mom, m * inv_root, g * inv_root, w))
            direction = [direction_bias] * 4
            magnitude = [magnitude_bias] * 4
            for j in range(32):
                coef = [table[j, i] for i in range(8)]
                for v in range(4):
                    pre = coef[5]
                    for i in range(5):
                        pre = pre + coef[i] * feats[v][i]
                    hidden = jnp.maximum(pre, 0.0)
                    direction[v] = direction[v] + coef[6] * hidden
                    magnitude[v] = magnitude[v] + coef[7] * hidden
            fresh = [
                weights[v] - STEP_SCALE * direction[v] * jnp.exp(EXP_SCALE * magnitude[v])
                for v in range(4)
            ]
            for n, at in enumerate(ats):
                both = jnp.concatenate([fresh[2 * n], fresh[2 * n + 1]], axis=0)
                gathered[my_rows, at] = both.astype(BF16)

        loop(tiles // 2, body)

    FROM_X = {3: 0, 1: 1}
    FROM_Z = {3: 2, 1: 3}
    X2, Z2 = 4, 5
    THEN_Z = {3: 6, 1: 7}
    THEN_X = {3: 8, 1: 9}
    LAST_X, LAST_Z = 10, 11
    FULL, H1, H2 = (0, wc), (0, half), (half, half)
    B1, A1, A2, B2 = ((i * quarter, quarter) for i in range(4))
    A12 = (quarter, half)

    def block(dx, dz):
        return (((z + dz) % 4) * 4 + (x + dx) % 4) * ROWS

    def push(row, k, part, device, sem):
        where = gathered.at[pl.ds(pl.multiple_of(row, ROWS), ROWS), cols(k, *part)]
        pltpu.make_async_remote_copy(
            src_ref=where,
            dst_ref=where,
            send_sem=gather_send.at[0],
            recv_sem=gather_recv.at[sem, k],
            device_id=device,
            device_id_type=MESH,
        ).start()

    def arrived(sem, k, rows, size):
        where = gathered.at[pl.ds(0, rows), pl.ds(0, size)]
        pltpu.make_async_copy(where, where, gather_recv.at[sem, k]).wait()

    def send_own(k):
        row = block(0, 0)
        push(row, k, FULL, on_x(1), FROM_X[3])
        push(row, k, FULL, on_x(3), FROM_X[1])
        push(row, k, FULL, on_z(1), FROM_Z[3])
        push(row, k, FULL, on_z(3), FROM_Z[1])

    def along_z(row, k):
        push(row, k, H1, on_z(1), THEN_Z[3])
        push(row, k, H1, on_z(3), THEN_Z[1])

    def along_x(row, k):
        push(row, k, H2, on_x(1), THEN_X[3])
        push(row, k, H2, on_x(3), THEN_X[1])

    def relay_near(k):
        arrived(FROM_X[3], k, ROWS, wc)
        push(block(3, 0), k, A12, on_x(1), X2)
        along_z(block(3, 0), k)
        arrived(FROM_X[1], k, ROWS, wc)
        push(block(1, 0), k, B1, on_x(3), X2)
        push(block(1, 0), k, B2, on_x(3), X2)
        along_z(block(1, 0), k)
        arrived(FROM_Z[3], k, ROWS, wc)
        push(block(0, 3), k, A12, on_z(1), Z2)
        along_x(block(0, 3), k)
        arrived(FROM_Z[1], k, ROWS, wc)
        push(block(0, 1), k, B1, on_z(3), Z2)
        push(block(0, 1), k, B2, on_z(3), Z2)
        along_x(block(0, 1), k)

    def relay_far(k):
        arrived(X2, k, ROWS, wc)
        along_z(block(2, 0), k)
        arrived(Z2, k, ROWS, wc)
        along_x(block(0, 2), k)

    def relay_last(k):
        arrived(THEN_Z[3], k, 3 * ROWS, half)
        for i in (1, 2, 3):
            push(block(i, 3), k, A1, on_z(1), LAST_Z)
        arrived(THEN_Z[1], k, 3 * ROWS, half)
        for i in (1, 2, 3):
            push(block(i, 1), k, B1, on_z(3), LAST_Z)
        arrived(THEN_X[3], k, 3 * ROWS, half)
        for i in (1, 2, 3):
            push(block(3, i), k, A2, on_x(1), LAST_X)
        arrived(THEN_X[1], k, 3 * ROWS, half)
        for i in (1, 2, 3):
            push(block(1, i), k, B2, on_x(3), LAST_X)

    def step(t):
        @pl.when(t < CHUNKS)
        def _():
            network(t)
            send_own(t)

        for lag, relay in zip(LAG, (relay_near, relay_far, relay_last)):

            @pl.when((t >= lag) & (t < CHUNKS + lag))
            def _(lag=lag, relay=relay):
                relay(t - lag)

    loop(CHUNKS + LAG[-1], step)

    def drain(k):
        arrived(LAST_X, k, 3 * ROWS, half)
        arrived(LAST_Z, k, 3 * ROWS, half)
        pair_copy(k).wait_send()
        for copy in (far_a, far_b, up_a, up_b, down_a, down_b):
            copy(k).wait_send()

    loop(CHUNKS, drain)
    for i in (1, 2, 3):
        sums_copy(sums_out, sums_in, 0, i, on_x(i)).wait_send()
        sums_copy(sums_out_z, sums_in_z, 1, i, on_z(i)).wait_send()
    sent = gathered.at[pl.ds(0, 15 * ROWS), :]
    pltpu.make_async_copy(sent, sent, gather_send.at[0]).wait()


def spread(table, j, i, value):
    table[j, i] = jnp.full((8, LANE), value, F32)


def offset(table, j, slope, bias, log_mom):
    table[j, 5] = log_mom * slope + bias


def per_device(grads, counts, weight, mom, second, in_weight, in_bias, out_weight, out_bias):
    rows, width = mom.shape[1:]
    hbm = pl.BlockSpec(memory_space=pltpu.HBM)
    smem = pl.BlockSpec(memory_space=pltpu.SMEM)
    vmem = pl.BlockSpec(memory_space=pltpu.VMEM)
    dma = pltpu.SemaphoreType.DMA
    gathered, new_mom, new_second = pl.pallas_call(
        functools.partial(kernel, width),
        out_shape=(
            pltpu.VMEM((rows * 16, width), BF16),
            pltpu.VMEM((rows, width), F32),
            pltpu.VMEM((rows, width), F32),
        ),
        in_specs=[vmem, smem, smem, smem, smem, hbm, hbm, hbm, hbm],
        out_specs=(vmem, vmem, vmem),
        scratch_shapes=[
            pltpu.VMEM((8, rows, width), BF16),
            pltpu.VMEM((rows, width), BF16),
            pltpu.VMEM((rows, width), F32),
            pltpu.VMEM((rows, width), F32),
            pltpu.VMEM((4, rows, width), BF16),
            pltpu.VMEM((4, rows, width), BF16),
            *[pltpu.VMEM((rows, width), BF16)] * 6,
            pltpu.VMEM((rows, width), F32),
            pltpu.VMEM((rows, width), F32),
            pltpu.VMEM((8, rows, LANE), F32),
            pltpu.VMEM((32, 8, 8, LANE), F32),
            pltpu.VMEM((2, 8, LANE), F32),
            pltpu.VMEM((3, 2, 8, LANE), F32),
            pltpu.VMEM((2, 8, LANE), F32),
            pltpu.VMEM((3, 2, 8, LANE), F32),
            dma((CHUNKS + 3,)),
            dma((CHUNKS,)),
            dma((CHUNKS,)),
            dma((6, CHUNKS)),
            dma((6, CHUNKS)),
            dma((2, 3)),
            dma((2, 3)),
            dma((1,)),
            dma((12, CHUNKS)),
        ],
        compiler_params=pltpu.CompilerParams(
            collective_id=0, has_side_effects=True, vmem_limit_bytes=36 << 20
        ),
        name="learned_step",
    )(counts, in_weight, in_bias, out_weight.T, out_bias, grads, weight, mom, second)
    return gathered[None], new_mom[None], new_second[None]


def solution(mesh):
    in_specs = (
        P("ep", None, "fs", None),
        P(),
        P("ep", "fs", None),
        P("ep", "fs", None),
        P("ep", "fs", None),
        P(),
        P(),
        P(),
        P(),
    )
    out_specs = (P("ep", None, None), P("ep", "fs", None), P("ep", "fs", None))
    return jax.shard_map(
        per_device, mesh=mesh, in_specs=in_specs, out_specs=out_specs, check_vma=False
    )
```

time: 247 us -> 97.7 us (0.40)
  waiting for transfers between devices: 110 us -> 0 us
  Pallas kernels: 0 us -> 83.1 us
  matrix products: 42 us -> 0 us
  other arithmetic: 35.8 us -> 0 us
  local copies, waits for them, and re-layouts: 29.4 us -> 13.7 us
  between operations: 15.4 us -> 0.66 us
  starting transfers between devices: 12.8 us -> 0 us
    pallas_call x0 -> x1, Pallas kernels: none -> 83.1 us  [per_device(): pl.pallas_call(functools.partial(kernel, width), out_shape=(pltpu.VMEM((r...]
    all_gather x1 -> x0, waiting for transfers between devices: 66.1 us -> none  [per_device(): gathered = lax.all_gather(updated[None], 'fs', axis=1, tiled=True)]
    all_to_all x2 -> x0, waiting for transfers between devices: 43.8 us -> none  [the longest x1 43.8 us: per_device(): lax.all_to_all(outgoing, 'ep', split_axis=1, concat_axis=0, tiled=True)]
    dot_general x16 -> x0, matrix products: 42 us -> none  [the longest x8 25.6 us: learned_step(): jnp.einsum('fh,fab->hab', in_weight, features, precision=lax.Precision.HI...]
    mul x8 -> x0, other arithmetic: 14.7 us -> none  [learned_step(): gradient * inv_root]
    another operation x11 -> x0, local copies, waits for them, and re-layouts: 12.7 us -> none  [the longest x8 8.98 us: learned_step(): jnp.stack([gradient / grad_norm, mom_next / mom_norm, mom_next * inv_root...]
    all_to_all x2 -> x0, starting transfers between devices: 12.6 us -> none  [the longest x1 7.88 us: from_everyone(): return lax.all_to_all(copies, axis, split_axis=0, concat_axis=0, tiled=True)]
    convert_element_type x18 -> x0, other arithmetic: 8.54 us -> none  [the longest x1 4.68 us: per_device(): outgoing = weighted.astype(jnp.bfloat16)]
  transfers between devices with their start and end apart: 3 -> 0, of which waited for: 2 -> 0; matrix products, arithmetic and copies ran while one was open for 4% -> 0% of each run, Pallas kernels for 0% -> 0%
where the time goes in v1:
time: 97.7 us; the launch traced here: 97.4 us
  Pallas kernels  83.1 us (85%)
  local copies, waits for them, and re-layouts  13.7 us (14%)
    pallas_call x1, Pallas kernels, per_device(): pl.pallas_call(functools.partial(kernel, width), out_shape=(pltpu.VMEM((r...  83.1 us
    unnamed x21, local copies, waits for them, and re-layouts  13.7 us

profile of v1, /device:TPU:0, one launch (start us, length us, event | category | flops | bytes accessed | tf_op | source)
XLA Modules:
  0.0 97.4 jit_solution(1205505124368715389)
XLA Ops:
  0.6 0.0 copy-start
  0.6 2.0 %copy-done = bf16[1,8,16,14336]{3,2,1,0:T(8,128)(2,1)S(1)} copy-done((bf16[1,8,16,14336]{3,2,1,0:T(8,128)(2,1)S(1)}, bf16[1,8,16,14336]{3,2,1,0:T(8,128)(2,1)}, u32[]{:S(2)}) %copy-start) | copy-done | bytes 3670040
  2.7 0.0 copy-start.1
  2.7 1.2 %copy-done.1 = f32[1,16,14336]{2,1,0:T(8,128)S(1)} copy-done((f32[1,16,14336]{2,1,0:T(8,128)S(1)}, f32[1,16,14336]{2,1,0:T(8,128)}, u32[]{:S(2)}) %copy-start.1) | copy-done | bytes 917528
  3.9 0.0 copy-start.2
  3.9 1.2 %copy-done.2 = f32[1,16,14336]{2,1,0:T(8,128)S(1)} copy-done((f32[1,16,14336]{2,1,0:T(8,128)S(1)}, f32[1,16,14336]{2,1,0:T(8,128)}, u32[]{:S(2)}) %copy-start.2) | copy-done | bytes 917528
  5.0 0.0 copy-start.3
  5.0 1.0 %copy-done.3 = bf16[1,16,14336]{2,1,0:T(8,128)(2,1)S(1)} copy-done((bf16[1,16,14336]{2,1,0:T(8,128)(2,1)S(1)}, bf16[1,16,14336]{2,1,0:T(8,128)(2,1)}, u32[]{:S(2)}) %copy-start.3) | copy-done | bytes 458776
  6.1 0.0 copy-start.4
  6.1 0.7 copy-done.4
  6.7 0.0 copy-start.5
  6.7 0.7 copy-done.5
  7.4 0.0 copy-start.6
  7.4 0.7 copy-done.6
  8.1 0.0 copy-start.7
  8.1 0.7 copy-done.7
  8.8 0.0 copy-start.8
  8.8 0.7 copy-done.8
  9.4 83.1 %learned_step.1 = (bf16[256,14336]{1,0:T(8,128)(2,1)S(1)}, f32[16,14336]{1,0:T(8,128)S(1)}, f32[16,14336]{1,0:T(8,128)S(1)}) custom-call(s32[8,8]{1,0:T(8,128)S(1)} %copy-done.4, f32[6,32]{1,0:T(8,128)S(1)} %copy-done.5, f32[32]{0:T(128)S(1)} %copy-done.7, f32[2,32]{1,0:T(2,128)S(1)} %bitcast.7, f32[2]{0:T(128)S(1)} %copy-done.8, ...), custom_call_target="tpu_custom_call" | custom-call | tf_op jit(solution)/shard_map/learned_step/pallas_call | solution.py:488
  92.5 3.1 %copy.15 = bf16[1,256,14336]{2,1,0:T(8,128)(2,1)} copy(bf16[1,256,14336]{2,1,0:T(8,128)(2,1)S(1)} %bitcast.4) | data formatting | bytes 14680064
  95.5 0.9 copy.16
  96.5 0.9 copy.17
Async XLA Ops:
  0.6 2.0 %copy-start = (bf16[1,8,16,14336]{3,2,1,0:T(8,128)(2,1)S(1)}, bf16[1,8,16,14336]{3,2,1,0:T(8,128)(2,1)}, u32[]{:S(2)}) copy-start(bf16[1,8,16,14336]{3,2,1,0:T(8,128)(2,1)} %grads_hbm.1) | copy-start | bytes 11010052
  2.7 1.2 %copy-start.1 = (f32[1,16,14336]{2,1,0:T(8,128)S(1)}, f32[1,16,14336]{2,1,0:T(8,128)}, u32[]{:S(2)}) copy-start(f32[1,16,14336]{2,1,0:T(8,128)} %mom_hbm.1) | copy-start | bytes 2752516
  3.9 1.2 %copy-start.2 = (f32[1,16,14336]{2,1,0:T(8,128)S(1)}, f32[1,16,14336]{2,1,0:T(8,128)}, u32[]{:S(2)}) copy-start(f32[1,16,14336]{2,1,0:T(8,128)} %second_hbm.1) | copy-start | bytes 2752516
  5.0 1.0 %copy-start.3 = (bf16[1,16,14336]{2,1,0:T(8,128)(2,1)S(1)}, bf16[1,16,14336]{2,1,0:T(8,128)(2,1)}, u32[]{:S(2)}) copy-start(bf16[1,16,14336]{2,1,0:T(8,128)(2,1)} %weight_hbm.1) | copy-start | bytes 1376260
  6.1 0.7 copy-start.4
  6.7 0.7 copy-start.5
  7.4 0.7 copy-start.6
  8.1 0.7 copy-start.7
  8.8 0.7 copy-start.8

commit v2 on v1

v2 whole, which is shorter than its diff:
```python
import functools

import jax
import jax.numpy as jnp
from jax import lax
from jax.experimental import pallas as pl
from jax.experimental.pallas import tpu as pltpu
from jax.sharding import PartitionSpec as P

MOMENTUM_DECAY = 0.9
SECOND_DECAY = 0.99
NORM_EPS = 1e-06
ROOT_EPS = 1e-08
STEP_SCALE = 0.2
EXP_SCALE = 0.5

ROWS = 16
LANE = 128
PARTS = 8
CHUNKS = 14
LAG = (3, 7, 14)
OTHERS = sorted(
    ((dx, dz) for dz in range(4) for dx in range(4) if dx or dz),
    key=lambda d: -min(d[0], 4 - d[0]) - min(d[1], 4 - d[1]),
)
STEPS = (2, 1, 3, 0)
MESH = pl.DeviceIdType.MESH
F32 = jnp.float32
BF16 = jnp.bfloat16

CODE_POWER = 6.0
CODE_SCALE = 2.0**14


def encode(x):
    y = jnp.exp(CODE_POWER * jnp.log(jnp.abs(x) * CODE_SCALE))
    return jnp.where(x < 0, -y, y).astype(BF16)


def decode(code):
    v = code.astype(F32)
    m = jnp.exp(jnp.log(jnp.abs(v)) * (1.0 / CODE_POWER)) * (1.0 / CODE_SCALE)
    return jnp.where(v < 0, -m, m)


def loop(n, body, unroll=1):
    def step(i, carry):
        body(i)
        return carry

    lax.fori_loop(0, n, step, 0, unroll=unroll)


def kernel(
    width,
    counts_hbm,
    in_weight_hbm,
    in_bias_hbm,
    out_weight_hbm,
    out_bias_hbm,
    grads_hbm,
    weight_hbm,
    mom_hbm,
    second_hbm,
    gathered,
    new_mom,
    new_second,
    counts,
    in_weight,
    in_bias,
    out_weight,
    out_bias,
    grads,
    weight,
    mom,
    second,
    to_pair,
    from_pair,
    far_out,
    far_in,
    up_out,
    up_in,
    down_out,
    down_in,
    own_sum,
    part_sum,
    shares,
    table,
    matrix,
    matrix_tail,
    hidden_a,
    hidden_b,
    sums_out,
    sums_in,
    load_sem,
    early_send,
    pair_recv,
    ring_recv,
    sums_sem,
    gather_send,
    gather_recv,
    last_recv,
):
    wc = width // CHUNKS
    half = wc // 2
    quarter = wc // 4
    ep = lax.axis_index("ep")
    fs = lax.axis_index("fs")
    y, core = ep // 2, ep % 2
    z, x = fs // 4, fs % 4

    def on_y(step):
        return {"ep": ((y + step) % 4) * 2 + core}

    def on_x(step):
        return {"fs": z * 4 + (x + step) % 4}

    def on_z(step):
        return {"fs": ((z + step) % 4) * 4 + x}

    partner = {"ep": y * 2 + (1 - core)}

    def await_bytes(sem, rows, size):
        where = gathered.at[pl.ds(0, rows), pl.ds(0, size)]
        pltpu.make_async_copy(where, where, sem).wait()

    def await_rows(sem, rows):
        await_bytes(sem, rows, width)

    def cols(k, start=0, size=None):
        return pl.ds(pl.multiple_of(k * wc + start, LANE), wc if size is None else size)

    def grads_load(k):
        return pltpu.make_async_copy(
            grads_hbm.at[0, :, :, cols(k)], grads.at[:, :, cols(k)], load_sem.at[k]
        )

    state_loads = [
        pltpu.make_async_copy(src.at[0], dst, load_sem.at[CHUNKS])
        for src, dst in ((weight_hbm, weight), (mom_hbm, mom), (second_hbm, second))
    ]
    barrier = pltpu.get_barrier_semaphore()
    peers = [partner, on_y(1), on_y(3)]
    peers += [{"fs": ((z + dz) % 4) * 4 + (x + dx) % 4} for dx, dz in OTHERS]
    for peer in peers:
        pl.semaphore_signal(barrier, inc=1, device_id=peer, device_id_type=MESH)

    small_loads = [
        pltpu.make_async_copy(src, dst, load_sem.at[CHUNKS + 1 + i])
        for i, (src, dst) in enumerate(
            (
                (counts_hbm, counts),
                (in_weight_hbm, in_weight),
                (in_bias_hbm, in_bias),
                (out_weight_hbm, out_weight),
                (out_bias_hbm, out_bias),
            )
        )
    ]
    small_loads[0].start()
    loop(CHUNKS, lambda k: grads_load(k).start())
    for load in small_loads[1:] + state_loads:
        load.start()

    small_loads[0].wait()
    counted = counts[...].astype(F32)
    share_table = counted / jnp.sum(counted, axis=0, keepdims=True)
    row_id = lax.broadcasted_iota(jnp.int32, (8, 8), 0)
    col_id = lax.broadcasted_iota(jnp.int32, (8, 8), 1)
    for i in range(8):
        c = core if i >= 4 else 1 - core
        e = ((y + STEPS[i % 4]) % 4) * 2 + c
        picked = jnp.where((row_id == ep) & (col_id == e), share_table, 0.0)
        one = jnp.sum(jnp.sum(picked, axis=1, keepdims=True), axis=0, keepdims=True)
        shares[i] = jnp.broadcast_to(one, (ROWS, LANE))

    with jax.named_scope("barrier"):
        pl.semaphore_wait(barrier, len(peers))

    tiles = wc // LANE
    half_tiles = half // LANE

    def tile(k, t):
        return pl.ds(pl.multiple_of(k * wc + t * LANE, LANE), LANE)

    def pair_copy(part, k):
        which = pl.ds(0, 1) if part == 0 else pl.ds(1, 3)
        return pltpu.make_async_remote_copy(
            src_ref=to_pair.at[which, :, cols(k)],
            dst_ref=from_pair.at[which, :, cols(k)],
            send_sem=early_send.at[0],
            recv_sem=pair_recv.at[part, k],
            device_id=partner,
            device_id_type=MESH,
        )

    def weigh(part, k):
        if part == 0:
            grads_load(k).wait()

        def body(t):
            at = tile(k, t)
            for n in (0,) if part == 0 else (1, 2, 3):
                e = ((y + STEPS[n]) % 4) * 2 + (1 - core)
                to_pair[n, :, at] = (grads[e, :, at].astype(F32) * shares[n]).astype(BF16)

        loop(tiles, body, unroll=4)
        pair_copy(part, k).start()

    with jax.named_scope("weigh"):
        loop(CHUNKS, functools.partial(weigh, 0))
        loop(CHUNKS, functools.partial(weigh, 1))

    def ring_copy(src, dst, kind, k, start, size, device):
        return pltpu.make_async_remote_copy(
            src_ref=src.at[:, cols(k, start, size)],
            dst_ref=dst.at[:, cols(k, start, size)],
            send_sem=early_send.at[0],
            recv_sem=ring_recv.at[min(kind, 2), k],
            device_id=device,
            device_id_type=MESH,
        )

    def far_a(k):
        return ring_copy(far_out, far_in, 0, k, 0, half, on_y(1))

    def far_b(k):
        return ring_copy(far_out, far_in, 1, k, half, half, on_y(3))

    def up_a(k):
        return ring_copy(up_out, up_in, 2, k, 0, half, on_y(1))

    def up_b(k):
        return ring_copy(up_out, up_in, 3, k, half, half, on_y(1))

    def down_a(k):
        return ring_copy(down_out, down_in, 4, k, 0, half, on_y(3))

    def down_b(k):
        return ring_copy(down_out, down_in, 5, k, half, half, on_y(3))

    def pair_sum(step, at):
        n = STEPS.index(step)
        e = ((y + step) % 4) * 2 + core
        mine = (grads[e, :, at].astype(F32) * shares[4 + n]).astype(BF16).astype(F32)
        return mine + from_pair[n, :, at].astype(F32)

    def sum_far(k):
        pair_copy(0, k).wait_recv()

        def far(t):
            at = tile(k, t)
            far_out[:, at] = encode(pair_sum(2, at))

        loop(tiles, far, unroll=2)
        far_a(k).start()
        far_b(k).start()

    def sum_near(k):
        pair_copy(1, k).wait_recv()

        def first(t):
            a, b = tile(k, t), tile(k, t + half_tiles)
            down_out[:, a] = encode(pair_sum(3, a))
            up_out[:, b] = encode(pair_sum(1, b))

        loop(half_tiles, first, unroll=2)
        up_b(k).start()
        down_a(k).start()

        def rest(t):
            a, b = tile(k, t), tile(k, t + half_tiles)
            part_sum[:, a] = pair_sum(1, a)
            part_sum[:, b] = pair_sum(3, b)
            own_sum[:, a] = pair_sum(0, a)
            own_sum[:, b] = pair_sum(0, b)

        loop(half_tiles, rest, unroll=2)

    with jax.named_scope("sum_pairs"):
        loop(CHUNKS, sum_far)
        loop(CHUNKS, sum_near)

    for load in small_loads[1:]:
        load.wait()
    lane = lax.broadcasted_iota(jnp.int32, (8, 2 * LANE), 1)
    same_row = lane % 8 == lax.broadcasted_iota(jnp.int32, (8, 2 * LANE), 0)
    feature = jnp.where(lane < 192, (lane % 32) // 8, jnp.where(lane < 216, 4, 5))
    group = lane // 32
    low = (group == 2) | ((lane >= 208) & (lane < 216))
    mid = (group == 1) | (group == 4) | ((lane >= 200) & (lane < 208))

    def fill_matrix(jj):
        parts = []
        for j in (2 * jj, 2 * jj + 1):
            value = jnp.zeros((8, 2 * LANE), F32)
            for i in range(5):
                value = jnp.where((feature == i) & same_row, in_weight[i, j], value)
            a, b, c = pieces(value)
            parts.append(jnp.where(low, c, jnp.where(mid, b, a)))
        both = jnp.concatenate(parts, axis=0)
        rows = pl.ds(pl.multiple_of(16 * jj, 16), 16)
        matrix[rows, :] = both.astype(BF16)
        matrix_tail[rows, :] = both[:, LANE:]
        for n, j in enumerate((2 * jj, 2 * jj + 1)):
            for i in range(2):
                table[j, i] = jnp.full((8, LANE), out_weight[i, j], F32)

    with jax.named_scope("fill"):
        loop(16, fill_matrix)

    def pass_on(k):
        far_a(k).wait_recv()

        def up(t):
            at = tile(k, t)
            up_out[:, at] = encode(part_sum[:, at] + decode(far_in[:, at]))

        loop(half_tiles, up, unroll=2)
        up_a(k).start()
        far_b(k).wait_recv()

        def down(t):
            at = tile(k, t + half_tiles)
            down_out[:, at] = encode(part_sum[:, at] + decode(far_in[:, at]))

        loop(half_tiles, down, unroll=2)
        down_b(k).start()

    with jax.named_scope("pass_on"):
        loop(CHUNKS, pass_on)

    await_rows(load_sem.at[CHUNKS], 5 * ROWS)

    def moments(k, sums):
        await_bytes(ring_recv.at[2, k], 2 * ROWS, wc)

        def body(t, sums):
            grad_sq, mom_sq = sums
            at = tile(k, t)
            gradient = own_sum[:, at] + decode(up_in[:, at]) + decode(down_in[:, at])
            mom_next = MOMENTUM_DECAY * mom[:, at] + (1.0 - MOMENTUM_DECAY) * gradient
            squared = gradient * gradient
            own_sum[:, at] = gradient
            new_mom[:, at] = mom_next
            new_second[:, at] = SECOND_DECAY * second[:, at] + (1.0 - SECOND_DECAY) * squared
            return grad_sq + squared, mom_sq + mom_next * mom_next

        return lax.fori_loop(0, tiles, body, sums, unroll=2)

    zero = jnp.zeros((ROWS, LANE), F32)
    with jax.named_scope("moments"):
        grad_sq, mom_sq = lax.fori_loop(0, CHUNKS, moments, (zero, zero))

    grad_sq = grad_sq[0:8] + grad_sq[8:16]
    mom_sq = mom_sq[0:8] + mom_sq[8:16]
    sums_out[...] = jnp.concatenate(
        [grad_sq[0:4] + grad_sq[4:8], mom_sq[0:4] + mom_sq[4:8]], axis=0
    )

    def sums_copy(dx, dz):
        i = dz * 4 + dx - 1
        return pltpu.make_async_remote_copy(
            src_ref=sums_out,
            dst_ref=sums_in.at[i],
            send_sem=sums_sem.at[0],
            recv_sem=sums_sem.at[1],
            device_id={"fs": ((z + dz) % 4) * 4 + (x + dx) % 4},
            device_id_type=MESH,
        )

    for dx, dz in OTHERS:
        sums_copy(dx, dz).start()
    total = sums_out[...]
    pltpu.make_async_copy(sums_in, sums_in, sums_sem.at[1]).wait()
    for i in range(15):
        total = total + sums_in[i]

    entries = float(ROWS * width * 16)
    total = jnp.sum(total, axis=1, keepdims=True)
    grad_var = jnp.sum(total[0:4], axis=0, keepdims=True) / entries + NORM_EPS
    mom_var = jnp.sum(total[4:8], axis=0, keepdims=True) / entries + NORM_EPS
    inv_grad = jnp.broadcast_to(lax.rsqrt(grad_var), (8, LANE))
    inv_mom = jnp.broadcast_to(lax.rsqrt(mom_var), (8, LANE))
    log_mom = jnp.broadcast_to(0.5 * jnp.log(mom_var), (8, LANE))

    tail_lane = lax.broadcasted_iota(jnp.int32, (8, LANE), 1) + LANE

    def fill_bias(jj):
        parts = []
        for j in (2 * jj, 2 * jj + 1):
            a, b, c = pieces(log_mom * in_weight[5, j] + in_bias[j])
            bias = jnp.where(tail_lane == 216, a, jnp.where(tail_lane == 217, b, c))
            parts.append(jnp.where((tail_lane >= 216) & (tail_lane < 219), bias, 0.0))
        rows = pl.ds(pl.multiple_of(16 * jj, 16), 16)
        both = matrix_tail[rows, :] + jnp.concatenate(parts, axis=0)
        matrix[rows, LANE:] = both.astype(BF16)

    loop(16, fill_bias, unroll=2)
    inv_grad = jnp.concatenate([inv_grad, inv_grad], axis=1)
    inv_mom = jnp.concatenate([inv_mom, inv_mom], axis=1)
    ones = jnp.ones((8, 2 * LANE), F32)
    direction_bias = jnp.full((8, LANE), out_bias[0], F32)
    magnitude_bias = jnp.full((8, LANE), out_bias[1], F32)

    my_rows = pl.ds(pl.multiple_of(fs * ROWS, ROWS), ROWS)

    last_pair = width // (2 * LANE) - 1

    def pair_at(p):
        return pl.ds(pl.multiple_of(p * (2 * LANE), 2 * LANE), 2 * LANE)

    def first_layer(p, hidden):
        at = pair_at(jnp.minimum(p, last_pair))
        w16 = weight[:, at].astype(F32)
        for n in range(2):
            rows = slice(8 * n, 8 * n + 8)
            g = own_sum[rows, at]
            m = new_mom[rows, at]
            w = w16[rows]
            inv_root = lax.rsqrt(new_second[rows, at] + ROOT_EPS)
            a1, b1, c1 = pieces(jnp.concatenate([g * inv_grad, m * inv_mom], axis=0))
            a2, b2, c2 = pieces(jnp.concatenate([m * inv_root, g * inv_root], axis=0))
            ww = jnp.concatenate([w, w], axis=0)
            wo = jnp.concatenate([w, ones], axis=0)
            stack = [a1, a2, a1, a2, a1, a2, b1, b2, b1, b2, c1, c2, ww, wo, ww, wo]
            right = jnp.concatenate([a.astype(BF16) for a in stack], axis=0)
            hidden[n] = jnp.dot(matrix[...], right, preferred_element_type=F32)

    def second_layer(p, hidden):
        at = pair_at(p)
        direction = [direction_bias] * 4
        magnitude = [magnitude_bias] * 4
        for j in range(32):
            to_direction, to_magnitude = table[j, 0], table[j, 1]
            for v in range(4):
                n, half_at = v // 2, v % 2
                h = hidden[n, 8 * j : 8 * j + 8, LANE * half_at : LANE * (half_at + 1)]
                h = jnp.maximum(h, 0.0)
                direction[v] = direction[v] + to_direction * h
                magnitude[v] = magnitude[v] + to_magnitude * h
        update = [
            STEP_SCALE * direction[v] * jnp.exp(EXP_SCALE * magnitude[v]) for v in range(4)
        ]
        rows = [jnp.concatenate(update[2 * n : 2 * n + 2], axis=1) for n in range(2)]
        fresh = weight[:, at].astype(F32) - jnp.concatenate(rows, axis=0)
        gathered[my_rows, at] = fresh.astype(BF16)

    pairs = tiles // 2

    def network(k):
        def body(t):
            p = k * pairs + 2 * t
            first_layer(p + 1, hidden_b)
            second_layer(p, hidden_a)
            first_layer(p + 2, hidden_a)
            second_layer(p + 1, hidden_b)

        loop(pairs // 2, body)

    first_layer(0, hidden_a)

    ONE, TWO, THEN = 0, 1, 2
    LAST = None
    FULL, H1, H2 = (0, wc), (0, half), (half, half)
    B1, A1, A2, B2 = ((i * quarter, quarter) for i in range(4))
    A12 = (quarter, half)

    def block(dx, dz):
        return (((z + dz) % 4) * 4 + (x + dx) % 4) * ROWS

    def push(row, k, part, device, sem):
        where = gathered.at[pl.ds(pl.multiple_of(row, ROWS), ROWS), cols(k, *part)]
        pltpu.make_async_remote_copy(
            src_ref=where,
            dst_ref=where,
            send_sem=gather_send.at[0],
            recv_sem=last_recv.at[0] if sem is LAST else gather_recv.at[sem, k],
            device_id=device,
            device_id_type=MESH,
        ).start()

    def arrived(sem, k, blocks=1):
        await_bytes(gather_recv.at[sem, k], blocks * ROWS, wc)

    def send_own(k):
        row = block(0, 0)
        push(row, k, FULL, on_x(1), ONE)
        push(row, k, FULL, on_x(3), ONE)
        push(row, k, FULL, on_z(1), ONE)
        push(row, k, FULL, on_z(3), ONE)

    def along_z(row, k):
        push(row, k, H1, on_z(1), THEN)
        push(row, k, H1, on_z(3), THEN)

    def along_x(row, k):
        push(row, k, H2, on_x(1), THEN)
        push(row, k, H2, on_x(3), THEN)

    def relay_near(k):
        arrived(ONE, k, 4)
        push(block(3, 0), k, A12, on_x(1), TWO)
        along_z(block(3, 0), k)
        push(block(1, 0), k, B1, on_x(3), TWO)
        push(block(1, 0), k, B2, on_x(3), TWO)
        along_z(block(1, 0), k)
        push(block(0, 3), k, A12, on_z(1), TWO)
        along_x(block(0, 3), k)
        push(block(0, 1), k, B1, on_z(3), TWO)
        push(block(0, 1), k, B2, on_z(3), TWO)
        along_x(block(0, 1), k)

    def relay_far(k):
        arrived(TWO, k, 2)
        along_z(block(2, 0), k)
        along_x(block(0, 2), k)

    def relay_last(k):
        arrived(THEN, k, 6)
        for i in (1, 2, 3):
            push(block(i, 3), k, A1, on_z(1), LAST)
            push(block(i, 1), k, B1, on_z(3), LAST)
            push(block(3, i), k, A2, on_x(1), LAST)
            push(block(1, i), k, B2, on_x(3), LAST)

    def step(t):
        @pl.when(t < CHUNKS)
        def _():
            with jax.named_scope("network"):
                network(t)
            send_own(t)

        for lag, relay in zip(LAG, (relay_near, relay_far, relay_last)):

            @pl.when((t >= lag) & (t < CHUNKS + lag))
            def _(lag=lag, relay=relay):
                relay(t - lag)

    with jax.named_scope("gather"):
        loop(CHUNKS + LAG[-1], step)

    with jax.named_scope("drain"):
        await_rows(last_recv.at[0], 3 * ROWS)
    await_rows(early_send.at[0], 7 * ROWS)
    pltpu.make_async_copy(sums_in, sums_in, sums_sem.at[0]).wait()
    with jax.named_scope("final"):
        await_rows(gather_send.at[0], 15 * ROWS)


def pieces(x):
    a = x.astype(BF16).astype(F32)
    b = (x - a).astype(BF16).astype(F32)
    return a, b, x - a - b


def write_out(gathered, new_mom, new_second, gathered_hbm, mom_hbm, second_hbm, sem):
    rows = gathered.shape[0] // PARTS
    copies = [
        pltpu.make_async_copy(
            gathered.at[pl.ds(i * rows, rows)], gathered_hbm.at[0, pl.ds(i * rows, rows)], sem.at[i]
        )
        for i in range(PARTS)
    ]
    copies.append(pltpu.make_async_copy(new_mom, mom_hbm.at[0], sem.at[PARTS]))
    copies.append(pltpu.make_async_copy(new_second, second_hbm.at[0], sem.at[PARTS + 1]))
    for copy in copies:
        copy.start()
    for copy in copies:
        copy.wait()


def per_device(grads, counts, weight, mom, second, in_weight, in_bias, out_weight, out_bias):
    rows, width = mom.shape[1:]
    hbm = pl.BlockSpec(memory_space=pltpu.HBM)
    vmem = pl.BlockSpec(memory_space=pltpu.VMEM)
    dma = pltpu.SemaphoreType.DMA
    gathered, new_mom, new_second = pl.pallas_call(
        functools.partial(kernel, width),
        out_shape=(
            pltpu.VMEM((rows * 16, width), BF16),
            pltpu.VMEM((rows, width), F32),
            pltpu.VMEM((rows, width), F32),
        ),
        in_specs=[hbm] * 9,
        out_specs=(vmem, vmem, vmem),
        scratch_shapes=[
            pltpu.VMEM((8, 8), jnp.int32),
            pltpu.SMEM((6, 32), F32),
            pltpu.SMEM((32,), F32),
            pltpu.SMEM((2, 32), F32),
            pltpu.SMEM((2,), F32),
            pltpu.VMEM((8, rows, width), BF16),
            pltpu.VMEM((rows, width), BF16),
            pltpu.VMEM((rows, width), F32),
            pltpu.VMEM((rows, width), F32),
            pltpu.VMEM((4, rows, width), BF16),
            pltpu.VMEM((4, rows, width), BF16),
            *[pltpu.VMEM((rows, width), BF16)] * 6,
            pltpu.VMEM((rows, width), F32),
            pltpu.VMEM((rows, width), F32),
            pltpu.VMEM((8, rows, LANE), F32),
            pltpu.VMEM((32, 2, 8, LANE), F32),
            pltpu.VMEM((256, 256), BF16),
            pltpu.VMEM((256, LANE), F32),
            pltpu.VMEM((2, 256, 256), F32),
            pltpu.VMEM((2, 256, 256), F32),
            pltpu.VMEM((8, LANE), F32),
            pltpu.VMEM((15, 8, LANE), F32),
            dma((CHUNKS + 6,)),
            dma((1,)),
            dma((2, CHUNKS)),
            dma((3, CHUNKS)),
            dma((2,)),
            dma((1,)),
            dma((3, CHUNKS)),
            dma((1,)),
        ],
        compiler_params=pltpu.CompilerParams(
            collective_id=0, has_side_effects=True, vmem_limit_bytes=36 << 20
        ),
        name="learned_step",
    )(*[
        pltpu.with_memory_space_constraint(a, pltpu.HBM)
        for a in (counts, in_weight, in_bias, out_weight.T, out_bias, grads, weight, mom, second)
    ])
    return pl.pallas_call(
        write_out,
        out_shape=tuple(
            jax.ShapeDtypeStruct((1, *a.shape), a.dtype) for a in (gathered, new_mom, new_second)
        ),
        in_specs=[vmem] * 3,
        out_specs=(hbm,) * 3,
        scratch_shapes=[dma((PARTS + 2,))],
        compiler_params=pltpu.CompilerParams(vmem_limit_bytes=1 << 20),
        name="write_out",
    )(gathered, new_mom, new_second)


def solution(mesh):
    in_specs = (
        P("ep", None, "fs", None),
        P(),
        P("ep", "fs", None),
        P("ep", "fs", None),
        P("ep", "fs", None),
        P(),
        P(),
        P(),
        P(),
    )
    out_specs = (P("ep", None, None), P("ep", "fs", None), P("ep", "fs", None))
    return jax.shard_map(
        per_device, mesh=mesh, in_specs=in_specs, out_specs=out_specs, check_vma=False
    )
```

time: 97.7 us -> 78.1 us (0.80)
  local copies, waits for them, and re-layouts: 13.7 us -> 0 us
  Pallas kernels: 83.1 us -> 77.3 us
    unnamed x21 -> x0, local copies, waits for them, and re-layouts: 13.7 us -> none
    pallas_call x1, Pallas kernels: 83.1 us -> 73.7 us  [per_device(): pl.pallas_call(functools.partial(kernel, width), out_shape=(pltpu.VMEM((r...]
    pallas_call x0 -> x1, Pallas kernels: none -> 3.63 us  [per_device(): pl.pallas_call(write_out, out_shape=tuple((jax.ShapeDtypeStruct((1, *a.sh...]
where the time goes in v2:
time: 78.1 us; the launch traced here: 77.9 us
  Pallas kernels  77.3 us (99%)
    pallas_call x1, Pallas kernels, per_device(): pl.pallas_call(functools.partial(kernel, width), out_shape=(pltpu.VMEM((r...  73.7 us
    pallas_call x1, Pallas kernels, per_device(): pl.pallas_call(write_out, out_shape=tuple((jax.ShapeDtypeStruct((1, *a.sh...  3.63 us

profile of v2, /device:TPU:0, one launch (start us, length us, event | category | flops | bytes accessed | tf_op | source)
XLA Modules:
  0.0 77.9 jit_solution(6489244059769286820)
XLA Ops:
  0.6 73.7 %learned_step.1 = (bf16[256,14336]{1,0:T(8,128)(2,1)S(1)}, f32[16,14336]{1,0:T(8,128)S(1)}, f32[16,14336]{1,0:T(8,128)S(1)}) custom-call(s32[8,8]{1,0:T(8,128)} %counts_hbm.1, f32[6,32]{1,0:T(8,128)} %in_weight_hbm.1, f32[32]{0:T(128)} %in_bias_hbm.1, f32[2,32]{1,0:T(2,128)} %bitcast.1, f32[2]{0:T(128)} %out_bias_hbm.1, bf16[1,8,16,14336]{3,2,1,0:T(8,128)(2,1)} %grads_hbm.1, ...), custom_call_target="tpu_custom_call" | custom-call | tf_op jit(solution)/shard_map/learned_step/pallas_call | solution.py:578
  74.3 3.6 %write_out.1 = (bf16[1,256,14336]{2,1,0:T(8,128)(2,1)}, f32[1,16,14336]{2,1,0:T(8,128)}, f32[1,16,14336]{2,1,0:T(8,128)}) custom-call(bf16[256,14336]{1,0:T(8,128)(2,1)S(1)} %get-tuple-element.6.gathered, f32[16,14336]{1,0:T(8,128)S(1)} %get-tuple-element.7.new_mom, f32[16,14336]{1,0:T(8,128)S(1)} %get-tuple-element.8.new_second), custom_call_target="tpu_custom_call" | custom-call | tf_op jit(solution)/shard_map/write_out/pallas_call | solution.py:627

commit v3 on v2

--- a/solution.py
+++ b/solution.py
@@ -16,7 +16,8 @@
 
 ROWS = 16
 LANE = 128
-PARTS = 8
+FIRST_CORE = 1
+GO_CHUNK = 13
 CHUNKS = 14
 LAG = (3, 7, 14)
 OTHERS = sorted(
@@ -93,6 +94,7 @@
     sums_out,
     sums_in,
     load_sem,
+    go,
     early_send,
     pair_recv,
     ring_recv,
@@ -121,22 +123,19 @@
     partner = {"ep": y * 2 + (1 - core)}
 
     def await_bytes(sem, rows, size):
-        where = gathered.at[pl.ds(0, rows), pl.ds(0, size)]
+        where = grads.at[pl.ds(0, rows // ROWS), :, pl.ds(0, size)]
         pltpu.make_async_copy(where, where, sem).wait()
 
-    def await_rows(sem, rows):
-        await_bytes(sem, rows, width)
 
     def cols(k, start=0, size=None):
         return pl.ds(pl.multiple_of(k * wc + start, LANE), wc if size is None else size)
 
-    def grads_load(k):
-        return pltpu.make_async_copy(
-            grads_hbm.at[0, :, :, cols(k)], grads.at[:, :, cols(k)], load_sem.at[k]
-        )
+    def grads_load(n):
+        pair = pl.ds(((y + STEPS[n]) % 4) * 2, 2)
+        return pltpu.make_async_copy(grads_hbm.at[0, pair], grads.at[pair], load_sem.at[n])
 
     state_loads = [
-        pltpu.make_async_copy(src.at[0], dst, load_sem.at[CHUNKS])
+        pltpu.make_async_copy(src.at[0], dst, load_sem.at[4])
         for src, dst in ((weight_hbm, weight), (mom_hbm, mom), (second_hbm, second))
     ]
     barrier = pltpu.get_barrier_semaphore()
@@ -146,7 +145,7 @@
         pl.semaphore_signal(barrier, inc=1, device_id=peer, device_id_type=MESH)
 
     small_loads = [
-        pltpu.make_async_copy(src, dst, load_sem.at[CHUNKS + 1 + i])
+        pltpu.make_async_copy(src, dst, load_sem.at[5 + i])
         for i, (src, dst) in enumerate(
             (
                 (counts_hbm, counts),
@@ -158,9 +157,8 @@
         )
     ]
     small_loads[0].start()
-    loop(CHUNKS, lambda k: grads_load(k).start())
-    for load in small_loads[1:] + state_loads:
-        load.start()
+    for n in range(4):
+        grads_load(n).start()
 
     small_loads[0].wait()
     counted = counts[...].astype(F32)
@@ -189,15 +187,12 @@
             src_ref=to_pair.at[which, :, cols(k)],
             dst_ref=from_pair.at[which, :, cols(k)],
             send_sem=early_send.at[0],
-            recv_sem=pair_recv.at[part, k],
+            recv_sem=pair_recv.at[k if part == 0 else CHUNKS],
             device_id=partner,
             device_id_type=MESH,
         )
 
     def weigh(part, k):
-        if part == 0:
-            grads_load(k).wait()
-
         def body(t):
             at = tile(k, t)
             for n in (0,) if part == 0 else (1, 2, 3):
@@ -208,15 +203,15 @@
         pair_copy(part, k).start()
 
     with jax.named_scope("weigh"):
+        grads_load(0).wait()
         loop(CHUNKS, functools.partial(weigh, 0))
-        loop(CHUNKS, functools.partial(weigh, 1))
 
     def ring_copy(src, dst, kind, k, start, size, device):
         return pltpu.make_async_remote_copy(
             src_ref=src.at[:, cols(k, start, size)],
             dst_ref=dst.at[:, cols(k, start, size)],
             send_sem=early_send.at[0],
-            recv_sem=ring_recv.at[min(kind, 2), k],
+            recv_sem=ring_recv.at[kind // 2 if kind < 2 else 1, k],
             device_id=device,
             device_id_type=MESH,
         )
@@ -257,8 +252,6 @@
         far_b(k).start()
 
     def sum_near(k):
-        pair_copy(1, k).wait_recv()
-
         def first(t):
             a, b = tile(k, t), tile(k, t + half_tiles)
             down_out[:, a] = encode(pair_sum(3, a))
@@ -278,7 +271,23 @@
         loop(half_tiles, rest, unroll=2)
 
     with jax.named_scope("sum_pairs"):
-        loop(CHUNKS, sum_far)
+        @pl.when(core == FIRST_CORE)
+        def _():
+            loop(CHUNKS, sum_far)
+
+        for n in (1, 2, 3):
+            grads_load(n).wait()
+        for load in small_loads[1:] + state_loads:
+            load.start()
+        loop(CHUNKS, functools.partial(weigh, 1))
+
+        @pl.when(core != FIRST_CORE)
+        def _():
+            pl.semaphore_wait(go, 1)
+            loop(CHUNKS, sum_far)
+
+        pair_near = from_pair.at[pl.ds(1, 3)]
+        pltpu.make_async_copy(pair_near, pair_near, pair_recv.at[CHUNKS]).wait()
         loop(CHUNKS, sum_near)
 
     for load in small_loads[1:]:
@@ -310,7 +319,11 @@
         loop(16, fill_matrix)
 
     def pass_on(k):
-        far_a(k).wait_recv()
+        @pl.when((core == FIRST_CORE) & (k == GO_CHUNK))
+        def _():
+            pl.semaphore_signal(go, inc=1, device_id=partner, device_id_type=MESH)
+
+        await_bytes(ring_recv.at[0, k], ROWS, wc)
 
         def up(t):
             at = tile(k, t)
@@ -318,7 +331,6 @@
 
         loop(half_tiles, up, unroll=2)
         up_a(k).start()
-        far_b(k).wait_recv()
 
         def down(t):
             at = tile(k, t + half_tiles)
@@ -330,10 +342,10 @@
     with jax.named_scope("pass_on"):
         loop(CHUNKS, pass_on)
 
-    await_rows(load_sem.at[CHUNKS], 5 * ROWS)
+    await_bytes(load_sem.at[4], 5 * ROWS, width)
 
     def moments(k, sums):
-        await_bytes(ring_recv.at[2, k], 2 * ROWS, wc)
+        await_bytes(ring_recv.at[1, k], 2 * ROWS, wc)
 
         def body(t, sums):
             grad_sq, mom_sq = sums
@@ -352,17 +364,15 @@
     with jax.named_scope("moments"):
         grad_sq, mom_sq = lax.fori_loop(0, CHUNKS, moments, (zero, zero))
 
-    grad_sq = grad_sq[0:8] + grad_sq[8:16]
-    mom_sq = mom_sq[0:8] + mom_sq[8:16]
     sums_out[...] = jnp.concatenate(
-        [grad_sq[0:4] + grad_sq[4:8], mom_sq[0:4] + mom_sq[4:8]], axis=0
+        [jnp.sum(grad_sq, axis=0, keepdims=True), jnp.sum(mom_sq, axis=0, keepdims=True)], axis=0
     )
+    sums_in[fs] = sums_out[...]
 
     def sums_copy(dx, dz):
-        i = dz * 4 + dx - 1
         return pltpu.make_async_remote_copy(
             src_ref=sums_out,
-            dst_ref=sums_in.at[i],
+            dst_ref=sums_in.at[fs],
             send_sem=sums_sem.at[0],
             recv_sem=sums_sem.at[1],
             device_id={"fs": ((z + dz) % 4) * 4 + (x + dx) % 4},
@@ -371,15 +381,17 @@
 
     for dx, dz in OTHERS:
         sums_copy(dx, dz).start()
-    total = sums_out[...]
-    pltpu.make_async_copy(sums_in, sums_in, sums_sem.at[1]).wait()
-    for i in range(15):
+    fifteen = sums_in.at[pl.ds(0, 15)]
+    with jax.named_scope("sums"):
+        pltpu.make_async_copy(fifteen, fifteen, sums_sem.at[1]).wait()
+    total = sums_in[0]
+    for i in range(1, 16):
         total = total + sums_in[i]
 
     entries = float(ROWS * width * 16)
     total = jnp.sum(total, axis=1, keepdims=True)
-    grad_var = jnp.sum(total[0:4], axis=0, keepdims=True) / entries + NORM_EPS
-    mom_var = jnp.sum(total[4:8], axis=0, keepdims=True) / entries + NORM_EPS
+    grad_var = total[0:1] / entries + NORM_EPS
+    mom_var = total[1:2] / entries + NORM_EPS
     inv_grad = jnp.broadcast_to(lax.rsqrt(grad_var), (8, LANE))
     inv_mom = jnp.broadcast_to(lax.rsqrt(mom_var), (8, LANE))
     log_mom = jnp.broadcast_to(0.5 * jnp.log(mom_var), (8, LANE))
@@ -403,7 +415,6 @@
     direction_bias = jnp.full((8, LANE), out_bias[0], F32)
     magnitude_bias = jnp.full((8, LANE), out_bias[1], F32)
 
-    my_rows = pl.ds(pl.multiple_of(fs * ROWS, ROWS), ROWS)
 
     last_pair = width // (2 * LANE) - 1
 
@@ -444,7 +455,7 @@
         ]
         rows = [jnp.concatenate(update[2 * n : 2 * n + 2], axis=1) for n in range(2)]
         fresh = weight[:, at].astype(F32) - jnp.concatenate(rows, axis=0)
-        gathered[my_rows, at] = fresh.astype(BF16)
+        gathered[z, x, :, at] = fresh.astype(BF16)
 
     pairs = tiles // 2
 
@@ -464,17 +475,19 @@
     LAST = None
     FULL, H1, H2 = (0, wc), (0, half), (half, half)
     B1, A1, A2, B2 = ((i * quarter, quarter) for i in range(4))
-    A12 = (quarter, half)
-
-    def block(dx, dz):
-        return (((z + dz) % 4) * 4 + (x + dx) % 4) * ROWS
-
-    def push(row, k, part, device, sem):
-        where = gathered.at[pl.ds(pl.multiple_of(row, ROWS), ROWS), cols(k, *part)]
+
+    def push(dx, dz, k, part, device, sem):
+        at = cols(k, *part)
+        if dx is None:
+            where = gathered.at[(z + dz) % 4, :, :, at]
+        elif dz is None:
+            where = gathered.at[:, (x + dx) % 4, :, at]
+        else:
+            where = gathered.at[(z + dz) % 4, (x + dx) % 4, :, at]
         pltpu.make_async_remote_copy(
             src_ref=where,
             dst_ref=where,
-            send_sem=gather_send.at[0],
+            send_sem=gather_send.at[1 if part == FULL or sem == TWO or 2 in (dx, dz) else 0],
             recv_sem=last_recv.at[0] if sem is LAST else gather_recv.at[sem, k],
             device_id=device,
             device_id_type=MESH,
@@ -484,45 +497,39 @@
         await_bytes(gather_recv.at[sem, k], blocks * ROWS, wc)
 
     def send_own(k):
-        row = block(0, 0)
-        push(row, k, FULL, on_x(1), ONE)
-        push(row, k, FULL, on_x(3), ONE)
-        push(row, k, FULL, on_z(1), ONE)
-        push(row, k, FULL, on_z(3), ONE)
-
-    def along_z(row, k):
-        push(row, k, H1, on_z(1), THEN)
-        push(row, k, H1, on_z(3), THEN)
-
-    def along_x(row, k):
-        push(row, k, H2, on_x(1), THEN)
-        push(row, k, H2, on_x(3), THEN)
+        for toward in (1, 3):
+            push(0, 0, k, FULL, on_x(toward), ONE)
+            push(0, 0, k, FULL, on_z(toward), ONE)
+
+    def along_z(dx, dz, k):
+        push(dx, dz, k, H1, on_z(1), THEN)
+        push(dx, dz, k, H1, on_z(3), THEN)
+
+    def along_x(dx, dz, k):
+        push(dx, dz, k, H2, on_x(1), THEN)
+        push(dx, dz, k, H2, on_x(3), THEN)
 
     def relay_near(k):
         arrived(ONE, k, 4)
-        push(block(3, 0), k, A12, on_x(1), TWO)
-        along_z(block(3, 0), k)
-        push(block(1, 0), k, B1, on_x(3), TWO)
-        push(block(1, 0), k, B2, on_x(3), TWO)
-        along_z(block(1, 0), k)
-        push(block(0, 3), k, A12, on_z(1), TWO)
-        along_x(block(0, 3), k)
-        push(block(0, 1), k, B1, on_z(3), TWO)
-        push(block(0, 1), k, B2, on_z(3), TWO)
-        along_x(block(0, 1), k)
+        push(3, 0, k, A1, on_x(1), TWO)
+        push(1, 0, k, B1, on_x(3), TWO)
+        push(0, 3, k, A2, on_z(1), TWO)
+        push(0, 1, k, B2, on_z(3), TWO)
+        for d in (3, 1):
+            along_z(d, 0, k)
+            along_x(0, d, k)
 
     def relay_far(k):
-        arrived(TWO, k, 2)
-        along_z(block(2, 0), k)
-        along_x(block(0, 2), k)
+        arrived(TWO, k)
+        along_z(2, 0, k)
+        along_x(0, 2, k)
 
     def relay_last(k):
         arrived(THEN, k, 6)
-        for i in (1, 2, 3):
-            push(block(i, 3), k, A1, on_z(1), LAST)
-            push(block(i, 1), k, B1, on_z(3), LAST)
-            push(block(3, i), k, A2, on_x(1), LAST)
-            push(block(1, i), k, B2, on_x(3), LAST)
+        push(None, 3, k, A1, on_z(1), LAST)
+        push(None, 1, k, B1, on_z(3), LAST)
+        push(3, None, k, A2, on_x(1), LAST)
+        push(1, None, k, B2, on_x(3), LAST)
 
     def step(t):
         @pl.when(t < CHUNKS)
@@ -541,11 +548,12 @@
         loop(CHUNKS + LAG[-1], step)
 
     with jax.named_scope("drain"):
-        await_rows(last_recv.at[0], 3 * ROWS)
-    await_rows(early_send.at[0], 7 * ROWS)
-    pltpu.make_async_copy(sums_in, sums_in, sums_sem.at[0]).wait()
+        await_bytes(last_recv.at[0], 4 * ROWS, width)
+    await_bytes(early_send.at[0], 7 * ROWS, width)
+    pltpu.make_async_copy(fifteen, fifteen, sums_sem.at[0]).wait()
     with jax.named_scope("final"):
-        await_rows(gather_send.at[0], 15 * ROWS)
+        await_bytes(gather_send.at[0], 8 * ROWS, width)
+        await_bytes(gather_send.at[1], 7 * ROWS, width)
 
 
 def pieces(x):
@@ -555,15 +563,14 @@
 
 
 def write_out(gathered, new_mom, new_second, gathered_hbm, mom_hbm, second_hbm, sem):
-    rows = gathered.shape[0] // PARTS
     copies = [
         pltpu.make_async_copy(
-            gathered.at[pl.ds(i * rows, rows)], gathered_hbm.at[0, pl.ds(i * rows, rows)], sem.at[i]
+            gathered.at[i // 4, i % 4], gathered_hbm.at[0, pl.ds(i * ROWS, ROWS)], sem.at[i]
         )
-        for i in range(PARTS)
+        for i in range(16)
     ]
-    copies.append(pltpu.make_async_copy(new_mom, mom_hbm.at[0], sem.at[PARTS]))
-    copies.append(pltpu.make_async_copy(new_second, second_hbm.at[0], sem.at[PARTS + 1]))
+    copies.append(pltpu.make_async_copy(new_mom, mom_hbm.at[0], sem.at[16]))
+    copies.append(pltpu.make_async_copy(new_second, second_hbm.at[0], sem.at[17]))
     for copy in copies:
         copy.start()
     for copy in copies:
@@ -578,7 +585,7 @@
     gathered, new_mom, new_second = pl.pallas_call(
         functools.partial(kernel, width),
         out_shape=(
-            pltpu.VMEM((rows * 16, width), BF16),
+            pltpu.VMEM((4, 4, rows, width), BF16),
             pltpu.VMEM((rows, width), F32),
             pltpu.VMEM((rows, width), F32),
         ),
@@ -605,14 +612,15 @@
             pltpu.VMEM((256, LANE), F32),
             pltpu.VMEM((2, 256, 256), F32),
             pltpu.VMEM((2, 256, 256), F32),
-            pltpu.VMEM((8, LANE), F32),
-            pltpu.VMEM((15, 8, LANE), F32),
-            dma((CHUNKS + 6,)),
+            pltpu.VMEM((2, LANE), F32),
+            pltpu.VMEM((16, 2, LANE), F32),
+            dma((10,)),
+            pltpu.SemaphoreType.REGULAR,
             dma((1,)),
+            dma((CHUNKS + 1,)),
             dma((2, CHUNKS)),
-            dma((3, CHUNKS)),
             dma((2,)),
-            dma((1,)),
+            dma((2,)),
             dma((3, CHUNKS)),
             dma((1,)),
         ],
@@ -627,11 +635,16 @@
     return pl.pallas_call(
         write_out,
         out_shape=tuple(
-            jax.ShapeDtypeStruct((1, *a.shape), a.dtype) for a in (gathered, new_mom, new_second)
+            jax.ShapeDtypeStruct(shape, dtype)
+            for shape, dtype in (
+                ((1, 16 * rows, width), BF16),
+                ((1, rows, width), F32),
+                ((1, rows, width), F32),
+            )
         ),
         in_specs=[vmem] * 3,
         out_specs=(hbm,) * 3,
-        scratch_shapes=[dma((PARTS + 2,))],
+        scratch_shapes=[dma((18,))],
         compiler_params=pltpu.CompilerParams(vmem_limit_bytes=1 << 20),
         name="write_out",
     )(gathered, new_mom, new_second)

time: 78.1 us -> 73 us (0.935)
  Pallas kernels: 77.3 us -> 72.2 us
    pallas_call x2, Pallas kernels: 77.3 us -> 72.2 us  [the longest x1 68.5 us: per_device(): pl.pallas_call(functools.partial(kernel, width), out_shape=(pltpu.VMEM((4...]
where the time goes in v3:
time: 73 us; the launch traced here: 72.9 us
  Pallas kernels  72.2 us (99%)
    pallas_call x1, Pallas kernels, per_device(): pl.pallas_call(functools.partial(kernel, width), out_shape=(pltpu.VMEM((4...  68.5 us
    pallas_call x1, Pallas kernels, per_device(): pl.pallas_call(write_out, out_shape=tuple((jax.ShapeDtypeStruct(shape, dt...  3.7 us

profile of v3, /device:TPU:0, one launch (start us, length us, event | category | flops | bytes accessed | tf_op | source)
XLA Modules:
  0.0 72.9 jit_solution(2212694324456050225)
XLA Ops:
  0.6 68.5 %learned_step.1 = (bf16[4,4,16,14336]{3,2,1,0:T(8,128)(2,1)S(1)}, f32[16,14336]{1,0:T(8,128)S(1)}, f32[16,14336]{1,0:T(8,128)S(1)}) custom-call(s32[8,8]{1,0:T(8,128)} %counts_hbm.1, f32[6,32]{1,0:T(8,128)} %in_weight_hbm.1, f32[32]{0:T(128)} %in_bias_hbm.1, f32[2,32]{1,0:T(2,128)} %bitcast.1, f32[2]{0:T(128)} %out_bias_hbm.1, ...), custom_call_target="tpu_custom_call" | custom-call | tf_op jit(solution)/shard_map/learned_step/pallas_call | solution.py:585
  69.2 3.7 %write_out.1 = (bf16[1,256,14336]{2,1,0:T(8,128)(2,1)}, f32[1,16,14336]{2,1,0:T(8,128)}, f32[1,16,14336]{2,1,0:T(8,128)}) custom-call(bf16[4,4,16,14336]{3,2,1,0:T(8,128)(2,1)S(1)} %get-tuple-element.6.gathered, f32[16,14336]{1,0:T(8,128)S(1)} %get-tuple-element.7.new_mom, f32[16,14336]{1,0:T(8,128)S(1)} %get-tuple-element.8.new_second), custom_call_target="tpu_custom_call" | custom-call | tf_op jit(solution)/shard_map/write_out/pallas_call | solution.py:635

commit v4 on v3

--- a/solution.py
+++ b/solution.py
@@ -17,9 +17,10 @@
 ROWS = 16
 LANE = 128
 FIRST_CORE = 1
+HEAD = 7
 GO_CHUNK = 13
 CHUNKS = 14
-LAG = (3, 7, 14)
+LAG = (3, 8, 14)
 OTHERS = sorted(
     ((dx, dz) for dz in range(4) for dx in range(4) if dx or dz),
     key=lambda d: -min(d[0], 4 - d[0]) - min(d[1], 4 - d[1]),
@@ -88,7 +89,8 @@
     shares,
     table,
     matrix,
-    matrix_tail,
+    base,
+    right,
     hidden_a,
     hidden_b,
     sums_out,
@@ -187,7 +189,7 @@
             src_ref=to_pair.at[which, :, cols(k)],
             dst_ref=from_pair.at[which, :, cols(k)],
             send_sem=early_send.at[0],
-            recv_sem=pair_recv.at[k if part == 0 else CHUNKS],
+            recv_sem=pair_recv.at[part, k],
             device_id=partner,
             device_id_type=MESH,
         )
@@ -205,6 +207,9 @@
     with jax.named_scope("weigh"):
         grads_load(0).wait()
         loop(CHUNKS, functools.partial(weigh, 0))
+        for n in (1, 2, 3):
+            grads_load(n).wait()
+        loop(HEAD, functools.partial(weigh, 1))
 
     def ring_copy(src, dst, kind, k, start, size, device):
         return pltpu.make_async_remote_copy(
@@ -252,6 +257,8 @@
         far_b(k).start()
 
     def sum_near(k):
+        pair_copy(1, k).wait_recv()
+
         def first(t):
             a, b = tile(k, t), tile(k, t + half_tiles)
             down_out[:, a] = encode(pair_sum(3, a))
@@ -275,48 +282,42 @@
         def _():
             loop(CHUNKS, sum_far)
 
-        for n in (1, 2, 3):
-            grads_load(n).wait()
         for load in small_loads[1:] + state_loads:
             load.start()
-        loop(CHUNKS, functools.partial(weigh, 1))
+        loop(CHUNKS - HEAD, lambda k: weigh(1, HEAD + k))
 
         @pl.when(core != FIRST_CORE)
         def _():
             pl.semaphore_wait(go, 1)
             loop(CHUNKS, sum_far)
 
-        pair_near = from_pair.at[pl.ds(1, 3)]
-        pltpu.make_async_copy(pair_near, pair_near, pair_recv.at[CHUNKS]).wait()
         loop(CHUNKS, sum_near)
 
     for load in small_loads[1:]:
         load.wait()
-    lane = lax.broadcasted_iota(jnp.int32, (8, 2 * LANE), 1)
-    same_row = lane % 8 == lax.broadcasted_iota(jnp.int32, (8, 2 * LANE), 0)
-    feature = jnp.where(lane < 192, (lane % 32) // 8, jnp.where(lane < 216, 4, 5))
-    group = lane // 32
-    low = (group == 2) | ((lane >= 208) & (lane < 216))
-    mid = (group == 1) | (group == 4) | ((lane >= 200) & (lane < 208))
-
-    def fill_matrix(jj):
-        parts = []
+    wide = (ROWS, LANE)
+    lane = lax.broadcasted_iota(jnp.int32, wide, 1)
+    same_row = lane % 8 == lax.broadcasted_iota(jnp.int32, wide, 0) % 8
+    first_unit = lax.broadcasted_iota(jnp.int32, wide, 0) < 8
+    feature = jnp.where(lane < 96, (lane % 32) // 8, jnp.where(lane < 120, 4, 5))
+    low = (lane >= 112) & (lane < 120)
+    mid = (lane // 32 == 1) | ((lane >= 104) & (lane < 112))
+
+    def unit_rows(jj):
+        return pl.ds(pl.multiple_of(16 * jj, 16), 16)
+
+    def fill_base(jj):
+        value = jnp.zeros(wide, F32)
+        for i in range(5):
+            pair = jnp.where(first_unit, in_weight[i, 2 * jj], in_weight[i, 2 * jj + 1])
+            value = jnp.where((feature == i) & same_row, pair, value)
+        base[unit_rows(jj), :] = value
         for j in (2 * jj, 2 * jj + 1):
-            value = jnp.zeros((8, 2 * LANE), F32)
-            for i in range(5):
-                value = jnp.where((feature == i) & same_row, in_weight[i, j], value)
-            a, b, c = pieces(value)
-            parts.append(jnp.where(low, c, jnp.where(mid, b, a)))
-        both = jnp.concatenate(parts, axis=0)
-        rows = pl.ds(pl.multiple_of(16 * jj, 16), 16)
-        matrix[rows, :] = both.astype(BF16)
-        matrix_tail[rows, :] = both[:, LANE:]
-        for n, j in enumerate((2 * jj, 2 * jj + 1)):
             for i in range(2):
                 table[j, i] = jnp.full((8, LANE), out_weight[i, j], F32)
 
     with jax.named_scope("fill"):
-        loop(16, fill_matrix)
+        loop(16, fill_base)
 
     def pass_on(k):
         @pl.when((core == FIRST_CORE) & (k == GO_CHUNK))
@@ -382,47 +383,14 @@
     for dx, dz in OTHERS:
         sums_copy(dx, dz).start()
     fifteen = sums_in.at[pl.ds(0, 15)]
-    with jax.named_scope("sums"):
-        pltpu.make_async_copy(fifteen, fifteen, sums_sem.at[1]).wait()
-    total = sums_in[0]
-    for i in range(1, 16):
-        total = total + sums_in[i]
-
-    entries = float(ROWS * width * 16)
-    total = jnp.sum(total, axis=1, keepdims=True)
-    grad_var = total[0:1] / entries + NORM_EPS
-    mom_var = total[1:2] / entries + NORM_EPS
-    inv_grad = jnp.broadcast_to(lax.rsqrt(grad_var), (8, LANE))
-    inv_mom = jnp.broadcast_to(lax.rsqrt(mom_var), (8, LANE))
-    log_mom = jnp.broadcast_to(0.5 * jnp.log(mom_var), (8, LANE))
-
-    tail_lane = lax.broadcasted_iota(jnp.int32, (8, LANE), 1) + LANE
-
-    def fill_bias(jj):
-        parts = []
-        for j in (2 * jj, 2 * jj + 1):
-            a, b, c = pieces(log_mom * in_weight[5, j] + in_bias[j])
-            bias = jnp.where(tail_lane == 216, a, jnp.where(tail_lane == 217, b, c))
-            parts.append(jnp.where((tail_lane >= 216) & (tail_lane < 219), bias, 0.0))
-        rows = pl.ds(pl.multiple_of(16 * jj, 16), 16)
-        both = matrix_tail[rows, :] + jnp.concatenate(parts, axis=0)
-        matrix[rows, LANE:] = both.astype(BF16)
-
-    loop(16, fill_bias, unroll=2)
-    inv_grad = jnp.concatenate([inv_grad, inv_grad], axis=1)
-    inv_mom = jnp.concatenate([inv_mom, inv_mom], axis=1)
+    last_pair = width // (2 * LANE) - 1
     ones = jnp.ones((8, 2 * LANE), F32)
-    direction_bias = jnp.full((8, LANE), out_bias[0], F32)
-    magnitude_bias = jnp.full((8, LANE), out_bias[1], F32)
-
-
-    last_pair = width // (2 * LANE) - 1
 
     def pair_at(p):
         return pl.ds(pl.multiple_of(p * (2 * LANE), 2 * LANE), 2 * LANE)
 
-    def first_layer(p, hidden):
-        at = pair_at(jnp.minimum(p, last_pair))
+    def prepare(p):
+        at = pair_at(p)
         w16 = weight[:, at].astype(F32)
         for n in range(2):
             rows = slice(8 * n, 8 * n + 8)
@@ -430,13 +398,54 @@
             m = new_mom[rows, at]
             w = w16[rows]
             inv_root = lax.rsqrt(new_second[rows, at] + ROOT_EPS)
-            a1, b1, c1 = pieces(jnp.concatenate([g * inv_grad, m * inv_mom], axis=0))
-            a2, b2, c2 = pieces(jnp.concatenate([m * inv_root, g * inv_root], axis=0))
+            a1, b1, _ = pieces(jnp.concatenate([g, m], axis=0))
+            a2, b2, _ = pieces(jnp.concatenate([m * inv_root, g * inv_root], axis=0))
             ww = jnp.concatenate([w, w], axis=0)
             wo = jnp.concatenate([w, ones], axis=0)
-            stack = [a1, a2, a1, a2, a1, a2, b1, b2, b1, b2, c1, c2, ww, wo, ww, wo]
-            right = jnp.concatenate([a.astype(BF16) for a in stack], axis=0)
-            hidden[n] = jnp.dot(matrix[...], right, preferred_element_type=F32)
+            for i, part in enumerate((a1, a2, b1, b2, ww, wo)):
+                right[p, n, 16 * i : 16 * i + 16, :] = part.astype(BF16)
+
+    with jax.named_scope("prepare"):
+        loop(last_pair + 1, prepare)
+    with jax.named_scope("sums"):
+        pltpu.make_async_copy(fifteen, fifteen, sums_sem.at[1]).wait()
+    total = sums_in[0]
+    for i in range(1, 16):
+        total = total + sums_in[i]
+
+    entries = float(ROWS * width * 16)
+    total = jnp.sum(total, axis=1, keepdims=True)
+    grad_var = total[0:1] / entries + NORM_EPS
+    mom_var = total[1:2] / entries + NORM_EPS
+    inv_grad = jnp.broadcast_to(lax.rsqrt(grad_var), wide)
+    inv_mom = jnp.broadcast_to(lax.rsqrt(mom_var), wide)
+    log_mom = jnp.broadcast_to(0.5 * jnp.log(mom_var), (ROWS, LANE))
+
+    scale = jnp.where(feature == 0, inv_grad, jnp.where(feature == 1, inv_mom, 1.0))
+
+    def fill_matrix(jj):
+        a, b, c = pieces(base[unit_rows(jj), :] * scale)
+        value = jnp.where(low, c, jnp.where(mid, b, a))
+        slope = jnp.where(first_unit, in_weight[5, 2 * jj], in_weight[5, 2 * jj + 1])
+        shift = jnp.where(first_unit, in_bias[2 * jj], in_bias[2 * jj + 1])
+        a, b, c = pieces(log_mom * slope + shift)
+        bias = jnp.where(lane == 120, a, jnp.where(lane == 121, b, c))
+        bias = jnp.where((lane >= 120) & (lane < 123), bias, 0.0)
+        matrix[unit_rows(jj), :] = (value + bias).astype(BF16)
+
+    with jax.named_scope("matrix"):
+        loop(16, fill_matrix, unroll=2)
+    direction_bias = jnp.full((8, LANE), out_bias[0], F32)
+    magnitude_bias = jnp.full((8, LANE), out_bias[1], F32)
+
+
+    def first_layer(p, hidden):
+        p = jnp.minimum(p, last_pair)
+        for n in range(2):
+            parts = [right[p, n, 16 * i : 16 * i + 16, :] for i in range(6)]
+            order = (0, 1, 0, 1, 2, 3, 4, 5)
+            whole = jnp.concatenate([parts[i] for i in order], axis=0)
+            hidden[n] = jnp.dot(matrix[...], whole, preferred_element_type=F32)
 
     def second_layer(p, hidden):
         at = pair_at(p)
@@ -608,8 +617,9 @@
             pltpu.VMEM((rows, width), F32),
             pltpu.VMEM((8, rows, LANE), F32),
             pltpu.VMEM((32, 2, 8, LANE), F32),
-            pltpu.VMEM((256, 256), BF16),
+            pltpu.VMEM((256, LANE), BF16),
             pltpu.VMEM((256, LANE), F32),
+            pltpu.VMEM((width // 256, 2, 96, 256), BF16),
             pltpu.VMEM((2, 256, 256), F32),
             pltpu.VMEM((2, 256, 256), F32),
             pltpu.VMEM((2, LANE), F32),
@@ -617,7 +627,7 @@
             dma((10,)),
             pltpu.SemaphoreType.REGULAR,
             dma((1,)),
-            dma((CHUNKS + 1,)),
+            dma((2, CHUNKS)),
             dma((2, CHUNKS)),
             dma((2,)),
             dma((2,)),

time: 73 us -> 72.5 us (level)
  no operation moved by 1% of the time
where the time goes in v4:
time: 72.5 us; the launch traced here: 72.4 us
  Pallas kernels  71.8 us (99%)
    pallas_call x1, Pallas kernels, per_device(): pl.pallas_call(functools.partial(kernel, width), out_shape=(pltpu.VMEM((4...  68.1 us
    pallas_call x1, Pallas kernels, per_device(): pl.pallas_call(write_out, out_shape=tuple((jax.ShapeDtypeStruct(shape, dt...  3.7 us

profile of v4, /device:TPU:0, one launch (start us, length us, event | category | flops | bytes accessed | tf_op | source)
XLA Modules:
  0.0 72.4 jit_solution(159796424392419454)
XLA Ops:
  0.6 68.1 %learned_step.1 = (bf16[4,4,16,14336]{3,2,1,0:T(8,128)(2,1)S(1)}, f32[16,14336]{1,0:T(8,128)S(1)}, f32[16,14336]{1,0:T(8,128)S(1)}) custom-call(s32[8,8]{1,0:T(8,128)} %counts_hbm.1, f32[6,32]{1,0:T(8,128)} %in_weight_hbm.1, f32[32]{0:T(128)} %in_bias_hbm.1, f32[2,32]{1,0:T(2,128)} %bitcast.1, f32[2]{0:T(128)} %out_bias_hbm.1, ...), custom_call_target="tpu_custom_call" | custom-call | tf_op jit(solution)/shard_map/learned_step/pallas_call | solution.py:594
  68.7 3.7 %write_out.1 = (bf16[1,256,14336]{2,1,0:T(8,128)(2,1)}, f32[1,16,14336]{2,1,0:T(8,128)}, f32[1,16,14336]{2,1,0:T(8,128)}) custom-call(bf16[4,4,16,14336]{3,2,1,0:T(8,128)(2,1)S(1)} %get-tuple-element.6.gathered, f32[16,14336]{1,0:T(8,128)S(1)} %get-tuple-element.7.new_mom, f32[16,14336]{1,0:T(8,128)S(1)} %get-tuple-element.8.new_second), custom_call_target="tpu_custom_call" | custom-call | tf_op jit(solution)/shard_map/write_out/pallas_call | solution.py:645
